TPU v7x, 32 devices: a whole 2x2x4 slice. The times are simulated.
32 devices in a mesh: dp: 8 (over z, y), mp: 4 (over x, core).
Axes of the slice: x: 2, y: 2, z: 4, core: 2. Of those that a mesh axis runs over, the one named last changes fastest.
Arguments:
- noise_blocks: bfloat16 [64, 12800], P('dp'), may hold values from -6 to 6
- data_blocks: bfloat16 [64, 12800], P('dp'), may hold values from -6 to 6
- destination: int32 [64], replicated, may hold values from 0 to 63, as said below
- utt_blocks: int32 [8, 4], P('dp'), may hold values from 1 to 4, 8 in all within a row
- span_start: int32 [8, 4], P('dp'), may hold values from 0 to 19
- span_size: int32 [8, 4], P('dp'), may hold values from 44 to 64
- timestep: int32 [8, 4], P('dp'), may hold values from 1 to 63
- in_weight: bfloat16 [200, 1024], replicated, may hold values from -0.4375 to 0.4375
- norm_gain: bfloat16 [1024], replicated, may hold values from 0.5 to 1.5
- qkv_weight: bfloat16 [1024, 3, 512], P(None, None, 'mp'), may hold values from -4 to 4
- out_proj: bfloat16 [512, 1024], P('mp'), may hold values from -0.25 to 0.25
- final_gain: bfloat16 [1024], replicated, may hold values from 0.25 to 1.75
- vel_weight: bfloat16 [1024, 100], replicated, may hold values from -0.1875 to 0.1875
Outputs:
- grad_qkv: float32 [1024, 3, 512], P('dp', None, 'mp')
- grad_out: float32 [512, 1024], P('mp', 'dp')
Inputs may be any that keep to these rules, and one draw needn't show every extreme that they name: `destination`: A permutation of the 64 bin positions; a device sends to each bin either none or exactly 1 of its blocks.
All inputs are finite; a program needn't handle non-finite values.
Results may differ from a plain program's by a relative error of at most 0.004.
Values may be sent and summed in bfloat16 or wider, within the bound.
A program may use at most 64 MiB of HBM per device.

v0:
```python
import jax
import jax.numpy as jnp
from jax import lax
from jax.sharding import PartitionSpec as P

HEAD_DIM = 64
BLOCK = 128


def frame_table(lengths, starts, sizes, steps, rows):
    ends = jnp.cumsum(lengths)
    frame = jnp.arange(rows, dtype=jnp.int32)
    block_index = frame // BLOCK
    segment = jnp.sum((block_index[:, None] >= ends[None, :]).astype(jnp.int32), axis=1)
    member = segment[:, None] == jnp.arange(lengths.shape[0], dtype=jnp.int32)[None, :]
    first = jnp.sum(jnp.where(member, (ends - lengths)[None, :], 0), axis=1) * BLOCK
    span = jnp.sum(jnp.where(member, lengths[None, :], 0), axis=1) * BLOCK
    lower = jnp.sum(jnp.where(member, starts[None, :], 0), axis=1)
    upper = lower + jnp.sum(jnp.where(member, sizes[None, :], 0), axis=1)
    inside = 64 * (frame - first)
    masked = ((inside >= lower * span) & (inside < upper * span)).astype(jnp.float32)
    level = jnp.sum(jnp.where(member, steps[None, :], 0), axis=1).astype(jnp.float32) / 64.0
    return (segment, masked, level)


def attend(query, keys, values, segment):
    rows, width = query.shape
    heads = width // HEAD_DIM
    block = min(512, rows)
    reach = min(4, rows // BLOCK // 2) * BLOCK
    window = min(rows, block + 2 * reach)
    blocks = rows // block
    query_blocks = query.reshape(blocks, block, heads, HEAD_DIM)
    segment_blocks = segment.reshape(blocks, block)
    firsts = jnp.clip(jnp.arange(blocks, dtype=jnp.int32) * block - reach, 0, rows - window)
    keyed = keys.reshape(rows, heads, HEAD_DIM)
    valued = values.reshape(rows, heads, HEAD_DIM)

    def one_block(item):
        query_block, segment_block, first = item
        scores = jnp.einsum(
            "qhd,khd->hqk", query_block, keyed, preferred_element_type=jnp.float32
        ) * HEAD_DIM ** (-0.5)
        scores = jnp.where((segment_block[:, None] == segment[None, :])[None], scores, -1e30)
        top = jnp.max(scores, axis=-1, keepdims=True)
        weights = jnp.exp(scores - top)
        probs = (weights / jnp.sum(weights, axis=-1, keepdims=True)).astype(jnp.bfloat16)
        return jnp.einsum(
            "hqk,khd->qhd", probs, valued, preferred_element_type=jnp.float32
        ).reshape(block, width)

    return lax.map(jax.checkpoint(one_block), (query_blocks, segment_blocks, firsts)).reshape(
        rows, width
    )


def shards(
    noise_blocks,
    data_blocks,
    destination,
    utt_blocks,
    span_start,
    span_size,
    timestep,
    in_weight,
    norm_gain,
    qkv_weight,
    out_proj,
    final_gain,
    vel_weight,
):
    sources = lax.axis_size("dp")
    here = lax.axis_index("dp")
    per_dev = noise_blocks.shape[0]
    depth = max(1, per_dev // sources)
    lanes_total = sources * depth
    table = destination.reshape(sources, per_dev)
    owner = table // per_dev
    order = jnp.arange(per_dev, dtype=jnp.int32)
    earlier = (owner[:, :, None] == owner[:, None, :]) & (
        order[None, None, :] < order[None, :, None]
    )
    rank = jnp.sum(earlier.astype(jnp.int32), axis=2)
    code = jnp.arange(sources, dtype=jnp.int32)[:, None] * depth + rank
    mine_owner = lax.dynamic_index_in_dim(owner, here, 0, keepdims=False)
    mine_rank = lax.dynamic_index_in_dim(rank, here, 0, keepdims=False)
    lanes = jnp.arange(lanes_total, dtype=jnp.int32)
    packing = (lanes[:, None] == (mine_owner * depth + mine_rank)[None, :]).astype(jnp.bfloat16)
    wanted = here * per_dev + order
    hit = table[None, :, :] == wanted[:, None, None]
    source_code = jnp.sum(jnp.where(hit, code[None, :, :], 0), axis=(1, 2))
    unpacking = (source_code[:, None] == lanes[None, :]).astype(jnp.bfloat16)

    def outgoing(blocks):
        sent = jnp.dot(packing, blocks, preferred_element_type=jnp.float32).astype(jnp.bfloat16)
        return sent.reshape(sources, depth, blocks.shape[1])

    def incoming(arrived):
        flat = arrived.reshape(lanes_total, arrived.shape[2])
        return jnp.dot(unpacking, flat, preferred_element_type=jnp.float32).astype(jnp.bfloat16)

    got_noise, got_data = (
        lax.all_to_all(outgoing(noise_blocks), "dp", split_axis=0, concat_axis=0, tiled=True),
        lax.all_to_all(outgoing(data_blocks), "dp", split_axis=0, concat_axis=0, tiled=True),
    )
    bin_noise = incoming(got_noise)
    bin_data = incoming(got_data)
    rows = per_dev * BLOCK
    mel = noise_blocks.shape[1] // BLOCK
    noise = bin_noise.reshape(rows, mel).astype(jnp.float32)
    data = bin_data.reshape(rows, mel).astype(jnp.float32)
    segment, masked, level = frame_table(
        utt_blocks[0], span_start[0], span_size[0], timestep[0], rows
    )
    noisy = (1.0 - level[:, None]) * noise + level[:, None] * data
    cond = data * (1.0 - masked[:, None])
    target = data - noise
    inputs = jnp.concatenate([noisy, cond], axis=1).astype(jnp.bfloat16)
    hidden0 = jnp.dot(inputs, in_weight, preferred_element_type=jnp.float32)
    scale = lax.rsqrt(jnp.mean(hidden0 * hidden0, axis=1, keepdims=True) + 1e-06)
    normed = (hidden0 * scale * norm_gain.astype(jnp.float32)[None, :]).astype(jnp.bfloat16)
    query = jnp.dot(normed, qkv_weight[:, 0, :], preferred_element_type=jnp.float32).astype(
        jnp.bfloat16
    )
    keys = jnp.dot(normed, qkv_weight[:, 1, :], preferred_element_type=jnp.float32).astype(
        jnp.bfloat16
    )
    values = jnp.dot(normed, qkv_weight[:, 2, :], preferred_element_type=jnp.float32).astype(
        jnp.bfloat16
    )
    heads_out, pullback = jax.vjp(lambda a, b, c: attend(a, b, c, segment), query, keys, values)
    attended = heads_out.astype(jnp.bfloat16)
    partial_mix = jnp.dot(attended, out_proj, preferred_element_type=jnp.float32)
    mixed = lax.psum(partial_mix.astype(jnp.bfloat16), "mp").astype(jnp.float32)
    hidden1 = (hidden0 + mixed).astype(jnp.bfloat16)
    wide1 = lax.optimization_barrier(hidden1).astype(jnp.float32)
    rscale = lax.rsqrt(jnp.mean(wide1 * wide1, axis=1, keepdims=True) + 1e-06)
    normalized = wide1 * rscale
    gain_out = final_gain.astype(jnp.float32)[None, :]
    final = (normalized * gain_out).astype(jnp.bfloat16)
    velocity = jnp.dot(final, vel_weight, preferred_element_type=jnp.float32)
    count = lax.psum(jnp.sum(masked), "dp")
    error = (2.0 * masked[:, None] * (velocity - target)).astype(jnp.bfloat16)
    grad_final = jnp.dot(error, vel_weight.T, preferred_element_type=jnp.float32)
    scaled = grad_final * gain_out
    back1 = (
        rscale * (scaled - normalized * jnp.mean(scaled * normalized, axis=1, keepdims=True))
    ).astype(jnp.bfloat16)
    back_att = jnp.dot(back1, out_proj.T, preferred_element_type=jnp.float32).astype(jnp.bfloat16)
    dquery, dkeys, dvalues = pullback(back_att.astype(jnp.float32))
    out_terms = jnp.dot(attended.T, back1, preferred_element_type=jnp.float32)
    qkv_terms = jnp.stack(
        [
            jnp.dot(normed.T, dquery, preferred_element_type=jnp.float32),
            jnp.dot(normed.T, dkeys, preferred_element_type=jnp.float32),
            jnp.dot(normed.T, dvalues, preferred_element_type=jnp.float32),
        ],
        axis=1,
    )
    summed_qkv, summed_out = (
        lax.psum_scatter(qkv_terms, "dp", scatter_dimension=0, tiled=True),
        lax.psum_scatter(out_terms, "dp", scatter_dimension=1, tiled=True),
    )
    return (summed_qkv / count, summed_out / count)


def solution(mesh):
    in_specs = (
        P("dp", None),
        P("dp", None),
        P(),
        P("dp", None),
        P("dp", None),
        P("dp", None),
        P("dp", None),
        P(),
        P(),
        P(None, None, "mp"),
        P("mp", None),
        P(),
        P(),
    )
    out_specs = (P("dp", None, "mp"), P("mp", "dp"))
    return jax.shard_map(shards, mesh=mesh, in_specs=in_specs, out_specs=out_specs, check_vma=False)
```

profile of v0, /device:TPU:0, one launch (start us, length us, event | category | flops | bytes accessed | tf_op | source)
XLA Modules:
  0.0 272.0 jit_solution(2920325727797531894)
XLA Ops:
  7.2 0.8 eq.126
  8.3 1.1 fusion.60
  9.9 0.8 reduce.1
  10.7 0.7 reshape.344
  11.4 7.3 %all-to-all-start = ((bf16[8,2,6400]{2,1,0:T(2,128)(2,1)}), bf16[8,2,6400]{2,1,0:T(2,128)(2,1)S(1)}, u32[]{:S(2)}, u32[]{:S(2)}) async-start(bf16[8,2,6400]{2,1,0:T(2,128)(2,1)} %reshape.344), calls=%async_computation | async-start | bytes 409600 | tf_op jit(solution)/shard_map/all_to_all | solution.py:103
  18.7 0.8 reduce-window.4
  20.3 0.8 select_reduce_fusion.5
  21.7 1.1 fusion.61
  22.9 0.8 reduce
  23.6 0.7 reshape.342
  24.4 2.4 all-to-all-done
  26.8 3.6 %all-to-all-start.1 = ((bf16[8,2,6400]{2,1,0:T(2,128)(2,1)}), bf16[8,2,6400]{2,1,0:T(2,128)(2,1)S(1)}, u32[]{:S(2)}, u32[]{:S(2)}) async-start(bf16[8,2,6400]{2,1,0:T(2,128)(2,1)} %reshape.342), calls=%async_computation.1 | async-start | bytes 409600 | tf_op jit(solution)/shard_map/all_to_all | solution.py:104
  32.4 0.9 reshape.336
  33.4 4.8 %all-to-all-done.1 = bf16[8,2,6400]{2,1,0:T(2,128)(2,1)S(1)} async-done(((bf16[8,2,6400]{2,1,0:T(2,128)(2,1)}), bf16[8,2,6400]{2,1,0:T(2,128)(2,1)S(1)}, u32[]{:S(2)}, u32[]{:S(2)}) %all-to-all-start.1) | async-done | bytes 204832 | tf_op jit(solution)/shard_map/all_to_all | solution.py:104
  38.6 0.9 reshape.337
  40.1 0.9 multiply_reduce_fusion
  41.4 1.3 copy-done.16
  42.7 0.8 convolution_convert_fusion.9
  44.1 1.2 convolution_convert_fusion.7
  45.5 1.0 copy.56
  46.5 17.6 %while.30 = (s32[]{:T(128)}, bf16[2,512,128]{2,1,0:T(8,128)(2,1)S(1)}, s32[2,512]{1,0:T(2,128)}, s32[1,1024]{1,0:T(1,128)S(1)}, bf16[2,512,2,64]{1,3,2,0:T(8,128...) while((s32[]{:T(128)}, bf16[2,512,128]{2,1,0:T(8,128)(2,1)S(1)}, ...), condition=%wide.region_13.14_spmd, body=%wide.region_10.13_spmd.sunk | while | flops 275252224 | bytes 11815545 | solution.py:52
  46.5 0.7 constant_dynamic-slice_fusion.6
  47.6 4.5 %fusion.178 = (f32[2,512]{1,0:T(2,128)S(1)}, f32[2,512,1024]{2,1,0:T(8,128)}) fusion(pred[512,1024]{1,0:T(8,128)(4,1)S(1)} %broadcast_compare_fusion.4, bf16[1024,2,64]{0,2,1:T(8,128)(2,1)S(1)} %get-tuple-element.617, bf16[2,512,2,64]{1,3,2,0:T(8,128)(2,1)} %get-tuple-element.616, s32[]{:T(128)} %get-tuple-element.604), kind=kOutput, calls=%fused_computation.176.clone.1 | convolution fusion | flops 138413056 | bytes 5116416 | tf_op jit(solution)/shard_map/jvp()/while/body/eval_jaxpr/sub | solution.py:46
  52.2 3.0 %fusion.179 = bf16[2,512,64]{1,2,0:T(8,128)(2,1)S(1)} fusion(bf16[1024,2,64]{0,2,1:T(8,128)(2,1)S(1)} %copy-done.19, f32[2,512,1024]{2,1,0:T(8,128)} %get-tuple-element.570, f32[2,512]{1,0:T(2,128)S(1)} %get-tuple-element.571), kind=kOutput, calls=%fused_computation.8.clone.1 | convolution fusion | flops 136314880 | bytes 4591616 | tf_op jit(solution)/shard_map/jvp()/while/body/eval_jaxpr/hqk,khd->qhd/dot_general | solution.py:48
  56.4 4.5 %fusion.178 = (f32[2,512]{1,0:T(2,128)S(1)}, f32[2,512,1024]{2,1,0:T(8,128)}) fusion(pred[512,1024]{1,0:T(8,128)(4,1)S(1)} %broadcast_compare_fusion.4, bf16[1024,2,64]{0,2,1:T(8,128)(2,1)S(1)} %get-tuple-element.617, bf16[2,512,2,64]{1,3,2,0:T(8,128)(2,1)} %get-tuple-element.616, s32[]{:T(128)} %get-tuple-element.604), kind=kOutput, calls=%fused_computation.176.clone.1 | convolution fusion | flops 138413056 | bytes 5116416 | tf_op jit(solution)/shard_map/jvp()/while/body/eval_jaxpr/sub | solution.py:46
  60.9 3.0 %fusion.179 = bf16[2,512,64]{1,2,0:T(8,128)(2,1)S(1)} fusion(bf16[1024,2,64]{0,2,1:T(8,128)(2,1)S(1)} %copy-done.19, f32[2,512,1024]{2,1,0:T(8,128)} %get-tuple-element.570, f32[2,512]{1,0:T(2,128)S(1)} %get-tuple-element.571), kind=kOutput, calls=%fused_computation.8.clone.1 | convolution fusion | flops 136314880 | bytes 4591616 | tf_op jit(solution)/shard_map/jvp()/while/body/eval_jaxpr/hqk,khd->qhd/dot_general | solution.py:48
  64.2 2.1 convolution_convert_fusion.5
  66.8 1.0 copy.54
  67.8 48.4 %all-reduce.2.cloned.1.call-done = bf16[1024,1024]{0,1:T(8,128)(2,1)} async-done(((bf16[1024,1024]{0,1:T(8,128)(2,1)}), bf16[1024,1024]{0,1:T(8,128)(2,1)}) %all-reduce.2.cloned.1.call-update) | async-done | bytes 2097168 | tf_op jit(solution)/shard_map/psum | solution.py:134
  116.2 3.6 %add_convert_fusion = bf16[1024,1024]{0,1:T(8,128)(2,1)S(1)} fusion(f32[1024,1024]{0,1:T(8,128)} %copy-done.4, bf16[1024,1024]{0,1:T(8,128)(2,1)} %all-reduce.2.cloned.1.call-done), kind=kLoop, calls=%fused_computation.88 | loop fusion | flops 3145728 | bytes 8388608 | tf_op jit(solution)/shard_map/convert_element_type | solution.py:135
  120.3 4.7 %fusion.66 = (f32[1024]{0:T(1024)S(1)}, f32[1024,1024]{0,1:T(8,128)}) fusion(bf16[1024,1024]{0,1:T(8,128)(2,1)S(1)} %add_convert_fusion, f32[1024]{0:T(1024)S(1)} %convert_element_type.200, f32[1024]{0:T(1024)S(1)} %add_rsqrt_fusion, bf16[1024,100]{0,1:T(8,128)(2,1)} %param.29, f32[1024,100]{0,1:T(8,128)} %copy.54, f32[1024,100]{0,1:T(8,128)S(1)} %copy.55, ...), kind=kOutput, calls=%fused_computation.83 | convolution fusion | flops 429276160 | bytes 7331840 | tf_op jit(solution)/shard_map/dot_general | solution.py:144
  125.0 3.7 %fusion.69 = bf16[1024,1024]{0,1:T(8,128)(2,1)S(1)} fusion(bf16[1024,1024]{0,1:T(8,128)(2,1)} %copy-done.7, f32[1024,1024]{0,1:T(8,128)} %get-tuple-element.459, f32[1024]{0:T(1024)S(1)} %broadcast_multiply_fusion, f32[1024]{0:T(1024)S(1)} %convert_element_type.200, f32[1024]{0:T(1024)S(1)} %add_rsqrt_fusion), kind=kLoop, calls=%fused_computation.86 | loop fusion | flops 7340032 | bytes 8400896 | tf_op jit(solution)/shard_map/convert_element_type | solution.py:148
  128.8 1.6 fusion.126
  130.4 0.8 convolution_convert_fusion.6
  131.2 0.7 broadcast_in_dim.194
  132.0 44.7 %while.31 = (s32[]{:T(128)}, bf16[1024,2,64]{0,2,1:T(8,128)(2,1)}, bf16[1024,2,64]{0,2,1:T(8,128)(2,1)}, bf16[2,512,2,64]{1,3,2,0:T(8,128)(2,1)}, bf16[2,512,2,6...) while((s32[]{:T(128)}, bf16[1024,2,64]{0,2,1:T(8,128)(2,1)}, ...), condition=%wide.region_23.24_spmd.clone, body=%wide.region_17.23_spmd.clone.sunk | while | flops 712179712 | bytes 109349352 | solution.py:52
  132.1 1.0 dynamic-slice_bitcast_fusion.2
  133.8 1.0 broadcast_compare_fusion.5
  134.9 2.1 fusion.187
  137.0 1.2 fusion.188
  138.2 2.8 %convert_reduce_fusion.5 = (f32[2,512]{1,0:T(2,128)S(1)}, pred[2,512,1024]{2,1,0:T(32,128)(4,1)S(1)}, f32[2,512]{1,0:T(2,128)S(1)}, bf16[2,512,1024]{2,1,0:T(8,128)(2,1)S(1)}) fusion(f32[2,512]{1,0:T(2,128)S(1)} %get-tuple-element.586, f32[2,512,1024]{2,1,0:T(8,128)S(1)} %get-tuple-element.587, pred[512,1024]{1,0:T(8,128)(4,1)S(1)} %broadcast_compare_fusion.5, ...), kind=kOutput, calls=%fused_computation.30.clone.1 | convolution fusion | flops 144701440 | bytes 8273920 | tf_op jit(solution)/shard_map/transpose(jvp())/while/body/eval_jaxpr/checkpoint/hqk,khd->qhd/dot_general | solution.py:48
  141.0 1.9 fusion.189
  143.0 1.9 copy-done.2
  144.9 2.2 fusion.192
  147.1 4.5 %fusion.191 = bf16[1024,2,64]{0,2,1:T(8,128)(2,1)} fusion(bf16[2,64,512]{2,1,0:T(8,128)(2,1)S(1)} %bitcast.163, f32[2,512]{1,0:T(2,128)} %copy-done.9, f32[2,512,1024]{2,1,0:T(8,128)} %copy-done.1, f32[2,512]{1,0:T(2,128)} %copy-done.11, pred[512,1024]{1,0:T(8,128)(4,1)S(1)} %broadcast_compare_fusion.5, ...), kind=kOutput, calls=%fused_computation.52.clone.1 | convolution fusion | flops 139722752 | bytes 5382145 | tf_op jit(solution)/shard_map/transpose(jvp())/while/body/eval_jaxpr/checkpoint/hqk,khd->qhd/dot_general | solution.py:48
  151.6 2.3 fusion.190
  154.0 0.9 dynamic-slice_bitcast_fusion.2
  155.6 1.0 broadcast_compare_fusion.5
  156.7 2.1 fusion.187
  158.8 1.2 fusion.188
  160.0 2.8 %convert_reduce_fusion.5 = (f32[2,512]{1,0:T(2,128)S(1)}, pred[2,512,1024]{2,1,0:T(32,128)(4,1)S(1)}, f32[2,512]{1,0:T(2,128)S(1)}, bf16[2,512,1024]{2,1,0:T(8,128)(2,1)S(1)}) fusion(f32[2,512]{1,0:T(2,128)S(1)} %get-tuple-element.586, f32[2,512,1024]{2,1,0:T(8,128)S(1)} %get-tuple-element.587, pred[512,1024]{1,0:T(8,128)(4,1)S(1)} %broadcast_compare_fusion.5, ...), kind=kOutput, calls=%fused_computation.30.clone.1 | convolution fusion | flops 144701440 | bytes 8273920 | tf_op jit(solution)/shard_map/transpose(jvp())/while/body/eval_jaxpr/checkpoint/hqk,khd->qhd/dot_general | solution.py:48
  162.9 1.9 fusion.189
  164.8 1.9 copy-done.2
  166.7 2.2 fusion.192
  168.9 4.6 %fusion.191 = bf16[1024,2,64]{0,2,1:T(8,128)(2,1)} fusion(bf16[2,64,512]{2,1,0:T(8,128)(2,1)S(1)} %bitcast.163, f32[2,512]{1,0:T(2,128)} %copy-done.9, f32[2,512,1024]{2,1,0:T(8,128)} %copy-done.1, f32[2,512]{1,0:T(2,128)} %copy-done.11, pred[512,1024]{1,0:T(8,128)(4,1)S(1)} %broadcast_compare_fusion.5, ...), kind=kOutput, calls=%fused_computation.52.clone.1 | convolution fusion | flops 139722752 | bytes 5382145 | tf_op jit(solution)/shard_map/transpose(jvp())/while/body/eval_jaxpr/checkpoint/hqk,khd->qhd/dot_general | solution.py:48
  173.5 3.2 %fusion.190 = bf16[1024,2,64]{0,2,1:T(8,128)(2,1)} fusion(bf16[512,2,64]{0,2,1:T(8,128)(2,1)S(1)} %dynamic-slice_bitcast_fusion.2, f32[2,512,1024]{2,1,0:T(8,128)S(1)} %copy-done.3, pred[2,512,1024]{2,1,0:T(32,128)(4,1)S(1)} %copy-done.22, f32[2,512]{1,0:T(2,128)S(1)} %copy-done.14, pred[512,1024]{1,0:T(8,128)(4,1)S(1)} %broadcast_compare_fusion.5, ...), kind=kOutput, calls=%fused_computation.53.clone.1 | convolution fusion | flops 138805248 | bytes 6426625 | tf_op jit(solution)/shard_map/transpose(jvp())/while/body/eval_jaxpr/checkpoint/qhd,khd->hqk/dot_general | solution.py:41
  176.7 1.3 copy.58
  178.0 0.7 convolution_bitcast_fusion.2
  178.7 1.7 convolution_bitcast_fusion.1
  181.1 1.3 pad_maximum_fusion
  182.4 21.8 %psum.15 = f32[]{:T(128)} all-reduce(f32[]{:T(128)} %get-tuple-element.442), channel_id=1, replica_groups=mesh['dp'=8,'mp'=4] {'dp'}, use_global_device_ids=true, to_apply=%region_26.27 | all-reduce | flops 1 | bytes 8 | tf_op jit(solution)/shard_map/psum | solution.py:142
  204.2 2.0 broadcast_divide_fusion.1
  206.2 57.0 %reduce-scatter.3.cloned.1.call-done = f32[128,3,128]{2,0,1:T(8,128)} async-done(((f32[1024,3,128]{2,0,1:T(8,128)}), f32[128,3,128]{2,0,1:T(8,128)}) %reduce-scatter.3.cloned.1.call-update) | async-done | bytes 196624 | tf_op jit(solution)/shard_map/reduce_scatter | solution.py:161
  263.3 2.2 broadcast_divide_fusion
  (128 shorter events, 11.6 us)
Async XLA Ops:
  7.2 32.9 %copy-start = (bf16[200,1024]{1,0:T(8,128)(2,1)S(1)}, bf16[200,1024]{1,0:T(8,128)(2,1)}, u32[]{:S(2)}) copy-start(bf16[200,1024]{1,0:T(8,128)(2,1)} %param.24) | copy-start | bytes 1228804
  11.4 15.4 %all-to-all-start = ((bf16[8,2,6400]{2,1,0:T(2,128)(2,1)}), bf16[8,2,6400]{2,1,0:T(2,128)(2,1)S(1)}, u32[]{:S(2)}, u32[]{:S(2)}) async-start(bf16[8,2,6400]{2,1,0:T(2,128)(2,1)} %reshape.344), calls=%async_computation | async-start | bytes 409600 | tf_op jit(solution)/shard_map/all_to_all | solution.py:103
  26.8 11.4 %all-to-all-start.1 = ((bf16[8,2,6400]{2,1,0:T(2,128)(2,1)}), bf16[8,2,6400]{2,1,0:T(2,128)(2,1)S(1)}, u32[]{:S(2)}, u32[]{:S(2)}) async-start(bf16[8,2,6400]{2,1,0:T(2,128)(2,1)} %reshape.342), calls=%async_computation.1 | async-start | bytes 409600 | tf_op jit(solution)/shard_map/all_to_all | solution.py:104
  30.4 85.8 %all-reduce.2.cloned.1.call-start = ((), (), s32[]{:S(2)}) async-start(), calls=%async_computation.4 | async-start | bytes 4194304 | tf_op jit(solution)/shard_map/psum | solution.py:134
  41.0 2.5 copy-start.4
  41.0 1.7 copy-start.16
  42.7 1.4 copy-start.5
  46.5 17.6 %copy-start.8 = (bf16[128,1024]{1,0:T(8,128)(2,1)S(1)}, bf16[128,1024]{1,0:T(8,128)(2,1)}, u32[]{:S(2)}) copy-start(bf16[128,1024]{1,0:T(8,128)(2,1)} %param.27) | copy-start | bytes 786436
  47.3 4.9 %copy-start.19 = (bf16[1024,2,64]{0,2,1:T(8,128)(2,1)S(1)}, bf16[1024,2,64]{0,2,1:T(8,128)(2,1)}, u32[]{:S(2)}) copy-start(bf16[1024,2,64]{0,2,1:T(8,128)(2,1)} %get-tuple-element.618) | copy-start | bytes 786436 | tf_op jit(solution)/shard_map/jvp()/while
  56.0 4.9 %copy-start.19 = (bf16[1024,2,64]{0,2,1:T(8,128)(2,1)S(1)}, bf16[1024,2,64]{0,2,1:T(8,128)(2,1)}, u32[]{:S(2)}) copy-start(bf16[1024,2,64]{0,2,1:T(8,128)(2,1)} %get-tuple-element.618) | copy-start | bytes 786436 | tf_op jit(solution)/shard_map/jvp()/while
  64.1 2.4 copy-start.17
  64.1 3.7 %copy-start.10 = (s32[1,1024]{1,0:T(1,128)}, s32[1,1024]{1,0:T(1,128)S(1)}, u32[]{:S(2)}) copy-start(s32[1,1024]{1,0:T(1,128)S(1)} %get-tuple-element.668) | copy-start | bytes 12292
  64.1 2.4 copy-start.15
  66.3 137.9 %reduce-scatter.5.cloned.1.call-start = ((), (), s32[]{:S(2)}) async-start(), calls=%async_computation.6 | async-start | bytes 589824 | tf_op jit(solution)/shard_map/reduce_scatter | solution.py:162
  119.8 5.2 %copy-start.7 = (bf16[1024,1024]{0,1:T(8,128)(2,1)}, bf16[1024,1024]{0,1:T(8,128)(2,1)S(1)}, u32[]{:S(2)}) copy-start(bf16[1024,1024]{0,1:T(8,128)(2,1)S(1)} %add_convert_fusion) | copy-start | bytes 6291460
  131.2 132.1 %reduce-scatter.3.cloned.1.call-start = ((), (), s32[]{:S(2)}) async-start(), calls=%async_computation.5 | async-start | bytes 1769472 | tf_op jit(solution)/shard_map/reduce_scatter | solution.py:161
  132.0 46.0 %copy-start.6 = (bf16[1024,1024]{0,1:T(8,128)(2,1)S(1)}, bf16[1024,1024]{0,1:T(8,128)(2,1)}, u32[]{:S(2)}) copy-start(bf16[1024,1024]{0,1:T(8,128)(2,1)} %copy-done.5) | copy-start | bytes 6291460
  134.9 3.3 %copy-start.20 = (bf16[1024,2,64]{0,2,1:T(8,128)(2,1)S(1)}, bf16[1024,2,64]{0,2,1:T(8,128)(2,1)}, u32[]{:S(2)}) copy-start(bf16[1024,2,64]{0,2,1:T(8,128)(2,1)} %get-tuple-element.589) | copy-start | bytes 786436 | tf_op jit(solution)/shard_map/transpose(jvp())/while
  137.0 4.0 %copy-start.1 = (f32[2,512,1024]{2,1,0:T(8,128)}, f32[2,512,1024]{2,1,0:T(8,128)S(1)}, u32[]{:S(2)}) copy-start(f32[2,512,1024]{2,1,0:T(8,128)S(1)} %get-tuple-element.587) | copy-start | bytes 12582916 | tf_op jit(solution)/shard_map/transpose(jvp())/while
  137.0 4.0 %copy-start.11 = (f32[2,512]{1,0:T(2,128)}, f32[2,512]{1,0:T(2,128)S(1)}, u32[]{:S(2)}) copy-start(f32[2,512]{1,0:T(2,128)S(1)} %get-tuple-element.586) | copy-start | bytes 12292 | tf_op jit(solution)/shard_map/transpose(jvp())/while
  138.2 2.9 %copy-start.9 = (f32[2,512]{1,0:T(2,128)}, f32[2,512]{1,0:T(2,128)S(1)}, u32[]{:S(2)}) copy-start(f32[2,512]{1,0:T(2,128)S(1)} %fusion.188) | copy-start | bytes 12292 | tf_op jit(solution)/shard_map/transpose(jvp())/while
  141.0 2.0 copy-start.21
  141.0 3.9 %copy-start.18 = (bf16[1024,2,64]{0,2,1:T(8,128)(2,1)S(1)}, bf16[1024,2,64]{0,2,1:T(8,128)(2,1)}, u32[]{:S(2)}) copy-start(bf16[1024,2,64]{0,2,1:T(8,128)(2,1)} %get-tuple-element.585) | copy-start | bytes 786436 | tf_op jit(solution)/shard_map/transpose(jvp())/while
  143.0 2.0 copy-start.2
  143.0 1.9 copy-start.13
  147.1 4.5 %copy-start.3 = (f32[2,512,1024]{2,1,0:T(8,128)S(1)}, f32[2,512,1024]{2,1,0:T(8,128)}, u32[]{:S(2)}) copy-start(f32[2,512,1024]{2,1,0:T(8,128)} %copy-done.2) | copy-start | bytes 12582916 | tf_op jit(solution)/shard_map/transpose(jvp())/while
  147.1 4.5 %copy-start.14 = (f32[2,512]{1,0:T(2,128)S(1)}, f32[2,512]{1,0:T(2,128)}, u32[]{:S(2)}) copy-start(f32[2,512]{1,0:T(2,128)} %copy-done.13) | copy-start | bytes 12292 | tf_op jit(solution)/shard_map/transpose(jvp())/while
  147.1 4.5 %copy-start.22 = (pred[2,512,1024]{2,1,0:T(32,128)(4,1)S(1)}, pred[2,512,1024]{2,1,0:T(32,128)(4,1)}, u32[]{:S(2)}) copy-start(pred[2,512,1024]{2,1,0:T(32,128)(4,1)} %copy-done.21) | copy-start | bytes 3145732 | tf_op jit(solution)/shard_map/transpose(jvp())/while
  156.7 3.3 %copy-start.20 = (bf16[1024,2,64]{0,2,1:T(8,128)(2,1)S(1)}, bf16[1024,2,64]{0,2,1:T(8,128)(2,1)}, u32[]{:S(2)}) copy-start(bf16[1024,2,64]{0,2,1:T(8,128)(2,1)} %get-tuple-element.589) | copy-start | bytes 786436 | tf_op jit(solution)/shard_map/transpose(jvp())/while
  158.8 4.0 %copy-start.1 = (f32[2,512,1024]{2,1,0:T(8,128)}, f32[2,512,1024]{2,1,0:T(8,128)S(1)}, u32[]{:S(2)}) copy-start(f32[2,512,1024]{2,1,0:T(8,128)S(1)} %get-tuple-element.587) | copy-start | bytes 12582916 | tf_op jit(solution)/shard_map/transpose(jvp())/while
  158.8 4.0 %copy-start.11 = (f32[2,512]{1,0:T(2,128)}, f32[2,512]{1,0:T(2,128)S(1)}, u32[]{:S(2)}) copy-start(f32[2,512]{1,0:T(2,128)S(1)} %get-tuple-element.586) | copy-start | bytes 12292 | tf_op jit(solution)/shard_map/transpose(jvp())/while
  160.0 2.9 %copy-start.9 = (f32[2,512]{1,0:T(2,128)}, f32[2,512]{1,0:T(2,128)S(1)}, u32[]{:S(2)}) copy-start(f32[2,512]{1,0:T(2,128)S(1)} %fusion.188) | copy-start | bytes 12292 | tf_op jit(solution)/shard_map/transpose(jvp())/while
  162.8 2.0 copy-start.21
  162.8 3.9 %copy-start.18 = (bf16[1024,2,64]{0,2,1:T(8,128)(2,1)S(1)}, bf16[1024,2,64]{0,2,1:T(8,128)(2,1)}, u32[]{:S(2)}) copy-start(bf16[1024,2,64]{0,2,1:T(8,128)(2,1)} %get-tuple-element.585) | copy-start | bytes 786436 | tf_op jit(solution)/shard_map/transpose(jvp())/while
  164.8 2.0 copy-start.2
  164.8 1.9 copy-start.13
  168.9 4.6 %copy-start.3 = (f32[2,512,1024]{2,1,0:T(8,128)S(1)}, f32[2,512,1024]{2,1,0:T(8,128)}, u32[]{:S(2)}) copy-start(f32[2,512,1024]{2,1,0:T(8,128)} %copy-done.2) | copy-start | bytes 12582916 | tf_op jit(solution)/shard_map/transpose(jvp())/while
  168.9 4.6 %copy-start.14 = (f32[2,512]{1,0:T(2,128)S(1)}, f32[2,512]{1,0:T(2,128)}, u32[]{:S(2)}) copy-start(f32[2,512]{1,0:T(2,128)} %copy-done.13) | copy-start | bytes 12292 | tf_op jit(solution)/shard_map/transpose(jvp())/while
  168.9 4.6 %copy-start.22 = (pred[2,512,1024]{2,1,0:T(32,128)(4,1)S(1)}, pred[2,512,1024]{2,1,0:T(32,128)(4,1)}, u32[]{:S(2)}) copy-start(pred[2,512,1024]{2,1,0:T(32,128)(4,1)} %copy-done.21) | copy-start | bytes 3145732 | tf_op jit(solution)/shard_map/transpose(jvp())/while
  176.7 3.7 %copy-start.12 = (bf16[1024,2,64]{0,2,1:T(8,128)(2,1)S(1)}, bf16[1024,2,64]{0,2,1:T(8,128)(2,1)}, u32[]{:S(2)}) copy-start(bf16[1024,2,64]{0,2,1:T(8,128)(2,1)} %get-tuple-element.274) | copy-start | bytes 786436
Sparse Core Ops, SparseCore 0:
  66.4 49.7 all-reduce.1
  131.3 63.3 reduce-scatter.4
  198.2 65.0 reduce-scatter.2
where the time goes:
time: 273 us; the launch traced here: 272 us
  waiting for transfers between devices  113 us (41%)
  matrix products  62 us (23%)
  other arithmetic  29 us (11%)
  blocking collectives  21.8 us (8%)
  local copies, waits for them, and re-layouts  20.8 us (8%)
  between operations  14.1 us (5%)
  starting transfers between devices  11.2 us (4%)
    reduce_scatter x1, waiting for transfers between devices, shards(): lax.psum_scatter(qkv_terms, 'dp', scatter_dimension=0, tiled=True)  57 us
    psum x1, waiting for transfers between devices, shards(): mixed = lax.psum(partial_mix.astype(jnp.bfloat16), 'mp').astype(jnp.float32)  48.4 us
    psum x1, blocking collectives, shards(): count = lax.psum(jnp.sum(masked), 'dp')  21.8 us
    dot_general x6, matrix products, one_block(): jnp.einsum('hqk,khd->qhd', probs, valued, preferred_element_type=jnp.floa...  20.7 us
    dot_general x6, matrix products, one_block(): jnp.einsum('qhd,khd->hqk', query_block, keyed, preferred_element_type=jnp...  14 us
    sub x2, matrix products, one_block(): weights = jnp.exp(scores - top)  9.01 us
    all_to_all x1, starting transfers between devices, shards(): lax.all_to_all(outgoing(noise_blocks), 'dp', split_axis=0, concat_axis=0,...  7.31 us
  transfers between devices with their start and end apart: 5, of which 4 were waited for; matrix products, arithmetic and copies ran while one was open for 22% of the time, Pallas kernels for 0%

commit v1 on v0

v1 whole, which is shorter than its diff:
```python
import functools

import jax
import jax.numpy as jnp
from jax import lax
from jax.experimental import pallas as pl
from jax.experimental.pallas import tpu as pltpu
from jax.sharding import PartitionSpec as P

HEAD_DIM = 64
BLOCK = 128
MESH = pl.DeviceIdType.MESH
VMEM = pl.BlockSpec(memory_space=pltpu.VMEM)
SMEM = pl.BlockSpec(memory_space=pltpu.SMEM)
F32, BF16 = jnp.float32, jnp.bfloat16
NT = (((1,), (1,)), ((), ()))
TN = (((0,), (0,)), ((), ()))


def dot(a, b, dims=(((1,), (0,)), ((), ()))):
    return lax.dot_general(a, b, dims, preferred_element_type=F32)


def params(**kw):
    return pltpu.CompilerParams(vmem_limit_bytes=56 * 2**20, **kw)


def greet(dp, mp, with_dp, with_mp):
    me, my = lax.axis_index("dp"), lax.axis_index("mp")
    barrier = pltpu.get_barrier_semaphore()
    n = 0
    if with_dp:
        for i in range(1, dp):
            pl.semaphore_signal(
                barrier, inc=1, device_id=(lax.rem(me + i, dp), my), device_id_type=MESH
            )
        n += dp - 1
    if with_mp:
        for i in range(1, mp):
            pl.semaphore_signal(
                barrier, inc=1, device_id=(me, lax.rem(my + i, mp)), device_id_type=MESH
            )
        n += mp - 1
    return lambda: pl.semaphore_wait(barrier, n)


def gather_mp(mp, src, dst_at, local, send, recv, fsend, frecv):
    me, my = lax.axis_index("dp"), lax.axis_index("mp")
    pair, side = my // 2, lax.rem(my, 2)
    mate = pair * 2 + 1 - side
    keep = pltpu.make_async_copy(src, dst_at(my), local)
    direct = []
    for c in range(1, mp // 2):
        far = lax.rem(pair + c, mp // 2) * 2 + side
        direct.append(
            pltpu.make_async_remote_copy(
                src, dst_at(my), send.at[c], recv.at[c], device_id=(me, far), device_id_type=MESH
            )
        )
    near = pltpu.make_async_remote_copy(
        src, dst_at(my), send.at[0], recv.at[0], device_id=(me, mate), device_id_type=MESH
    )

    def start():
        for d in direct:
            d.start()
        near.start()
        keep.start()

    def finish():
        onward = []
        for c, d in enumerate(direct, 1):
            d.wait_recv()
            origin = lax.rem(pair + mp // 2 - c, mp // 2) * 2 + side
            f = pltpu.make_async_remote_copy(
                dst_at(origin), dst_at(origin), fsend.at[c], frecv.at[c],
                device_id=(me, mate), device_id_type=MESH,
            )
            f.start()
            onward.append(f)
        near.wait()
        keep.wait()
        for d in direct:
            d.wait_send()
        for f in onward:
            f.wait()

    return start, finish


def load_kernel(
    dp, mp, pick_ref, from_ref, utt_ref, start_ref, size_ref, x_ref, w_ref,
    bin_ref, full_ref, count_ref,
    stage, got, tally, send, recv, csend, crecv, local, ssend, srecv, fsend, frecv,
):
    me, my = lax.axis_index("dp"), lax.axis_index("mp")
    wait = greet(dp, mp, True, True)
    for i in range(dp):
        stage[i] = x_ref[pick_ref[lax.rem(me + i, dp)]]
    count = jnp.int32(0)
    for u in range(utt_ref.shape[1]):
        low = start_ref[0, u]
        high = jnp.minimum(low + size_ref[0, u], 64)
        count += (high - low) * utt_ref[0, u] * (BLOCK // 64)
    tally[me] = jnp.full(tally.shape[1:], count, jnp.int32).astype(F32)
    wait()
    rows = w_ref.shape[0]
    start, finish = gather_mp(
        mp, w_ref, lambda i: full_ref.at[pl.ds(pl.multiple_of(i * rows, rows), rows)],
        local, ssend, srecv, fsend, frecv,
    )
    copies = []
    for i in range(1, dp):
        to = lax.rem(me + i, dp)
        copies.append(
            pltpu.make_async_remote_copy(
                stage.at[i], got.at[me], send.at[i], recv.at[i],
                device_id=(to, my), device_id_type=MESH,
            )
        )
        copies.append(
            pltpu.make_async_remote_copy(
                tally.at[me], tally.at[me], csend.at[i], crecv.at[i],
                device_id=(to, my), device_id_type=MESH,
            )
        )
    for c in copies:
        c.start()
    start()
    got[me] = stage[0]
    finish()
    for c in copies:
        c.wait()
    for j in range(bin_ref.shape[0]):
        bin_ref[j] = got[from_ref[j]]
    count_ref[...] = jnp.sum(tally[...], axis=0)


def gather_kernel(dp, mp, a_ref, out_ref, local, send, recv, fsend, frecv):
    greet(dp, mp, False, True)()
    start, finish = gather_mp(mp, a_ref, lambda i: out_ref.at[i], local, send, recv, fsend, frecv)
    start()
    finish()


def reduce_kernel(dp, mp, qkv_ref, o_ref, qkv_out, o_out, gq, go, sq, rq, so, ro):
    me, my = lax.axis_index("dp"), lax.axis_index("mp")
    greet(dp, mp, True, False)()
    rows = qkv_out.shape[0]

    def part(ref, i):
        return ref.at[pl.ds(pl.multiple_of(i * rows, rows), rows)]

    copies = []
    for i in range(1, dp):
        to = lax.rem(me + i, dp)
        for ref, got, s, r in ((qkv_ref, gq, sq, rq), (o_ref, go, so, ro)):
            copies.append(
                pltpu.make_async_remote_copy(
                    part(ref, to), got.at[i - 1], s.at[i], r.at[i],
                    device_id=(to, my), device_id_type=MESH,
                )
            )
    for c in copies:
        c.start()
    qkv_out[...] = part(qkv_ref, me)[...].astype(F32)
    o_out[...] = part(o_ref, me)[...].astype(F32)
    for i in range(1, dp):
        copies[2 * i - 2].wait()
        copies[2 * i - 1].wait()
        qkv_out[...] += gq[i - 1].astype(F32)
        o_out[...] += go[i - 1].astype(F32)


def segment_of(utt_ref, b):
    first, length, at = jnp.int32(0), jnp.int32(0), jnp.int32(0)
    for u in range(utt_ref.shape[1]):
        n = utt_ref[0, u]
        inside = (b >= at) & (b < at + n)
        first = jnp.where(inside, at, first)
        length = jnp.where(inside, n, length)
        at = at + n
    return first, length


def head_masks(width):
    lane = lax.broadcasted_iota(jnp.int32, (1, width), 1) // HEAD_DIM
    return [lane == h for h in range(width // HEAD_DIM)]


def for_blocks(utt_ref, blocks, longest, body):
    def step(b, _):
        first, length = segment_of(utt_ref, b)
        rows = pl.ds(pl.multiple_of(b * BLOCK, BLOCK), BLOCK)
        for n in range(1, longest + 1):
            @pl.when(length == n)
            def _():
                body(rows, pl.ds(pl.multiple_of(first * BLOCK, BLOCK), n * BLOCK))
        return 0

    lax.fori_loop(0, blocks, step, 0)


def softmax(s):
    e = jnp.exp(s - jnp.max(s, axis=1, keepdims=True))
    return e / jnp.sum(e, axis=1, keepdims=True)


def attend_kernel(longest, utt_ref, q_ref, k_ref, v_ref, out_ref):
    masks = head_masks(q_ref.shape[1])

    def body(rows, keys):
        q, k, v = q_ref[rows] * BF16(HEAD_DIM**-0.5), k_ref[keys], v_ref[keys]
        out = None
        for m in masks:
            p = softmax(dot(jnp.where(m, q, BF16(0)), k, NT)).astype(BF16)
            o = dot(p, v)
            out = o if out is None else jnp.where(m, o, out)
        out_ref[rows] = out.astype(BF16)

    for_blocks(utt_ref, q_ref.shape[0] // BLOCK, longest, body)


def pullback_kernel(longest, utt_ref, q_ref, k_ref, v_ref, do_ref, d_ref, dk, dv):
    width = q_ref.shape[1]
    masks = head_masks(width)
    dk[...] = jnp.zeros_like(dk)
    dv[...] = jnp.zeros_like(dv)
    scale = HEAD_DIM**-0.5

    def body(rows, keys):
        q, k, v = q_ref[rows] * BF16(scale), k_ref[keys], v_ref[keys]
        do = do_ref[rows]
        dq = None
        for m in masks:
            qh = jnp.where(m, q, BF16(0))
            doh = jnp.where(m, do, BF16(0))
            p = softmax(dot(qh, k, NT))
            dp = dot(doh, v, NT).astype(BF16).astype(F32)
            ds = (p * (dp - jnp.sum(dp * p, axis=1, keepdims=True))).astype(BF16)
            g = dot(ds, k)
            dq = g if dq is None else jnp.where(m, g, dq)
            dk[keys] += dot(ds, qh, TN)
            dv[keys] += dot(p.astype(BF16), doh, TN)
        d_ref[rows, :width] = (dq * scale).astype(BF16)

    for_blocks(utt_ref, q_ref.shape[0] // BLOCK, longest, body)
    d_ref[:, width : 2 * width] = dk[...].astype(BF16)
    d_ref[:, 2 * width :] = dv[...].astype(BF16)


def shards(
    dp, mp, noise_blocks, data_blocks, destination, utt_blocks, span_start, span_size, timestep,
    in_weight, norm_gain, qkv_weight, out_proj, final_gain, vel_weight,
):
    me = lax.axis_index("dp")
    per_dev = noise_blocks.shape[0]
    rows = per_dev * BLOCK
    mel = noise_blocks.shape[1] // BLOCK
    features = in_weight.shape[1]
    width = qkv_weight.shape[2]
    longest = min(4, per_dev)
    order = jnp.arange(per_dev, dtype=jnp.int32)
    mine = lax.dynamic_slice_in_dim(destination, me * per_dev, per_dev) // per_dev
    pick = jnp.sum(
        jnp.where(mine[None, :] == jnp.arange(dp, dtype=jnp.int32)[:, None], order[None, :], 0), axis=1
    )
    source = jnp.arange(destination.shape[0], dtype=jnp.int32) // per_dev
    origin = jnp.sum(
        jnp.where(destination[None, :] == (me * per_dev + order)[:, None], source[None, :], 0), axis=1
    )
    frames = jnp.concatenate(
        [noise_blocks.reshape(per_dev, BLOCK, mel), data_blocks.reshape(per_dev, BLOCK, mel)], axis=2
    )
    dma = pltpu.SemaphoreType.DMA
    bins, out_full, count = pl.pallas_call(
        functools.partial(load_kernel, dp, mp),
        out_shape=(
            jax.ShapeDtypeStruct(frames.shape, BF16),
            jax.ShapeDtypeStruct((mp * width, features), BF16),
            jax.ShapeDtypeStruct((8, 128), F32),
        ),
        in_specs=[SMEM] * 5 + [VMEM] * 2,
        out_specs=(VMEM,) * 3,
        scratch_shapes=[
            pltpu.VMEM((dp,) + frames.shape[1:], BF16),
            pltpu.VMEM((dp,) + frames.shape[1:], BF16),
            pltpu.VMEM((dp, 8, 128), F32),
            dma((dp,)), dma((dp,)), dma((dp,)), dma((dp,)), dma(()),
            dma((mp,)), dma((mp,)), dma((mp,)), dma((mp,)),
        ],
        compiler_params=params(collective_id=0, has_side_effects=True),
        name="load_blocks",
    )(pick, origin, utt_blocks, span_start, span_size, frames, out_proj)

    lengths = utt_blocks[0]
    ends = jnp.cumsum(lengths)
    frame = jnp.arange(rows, dtype=jnp.int32)
    block = frame // BLOCK
    member = (block[:, None] >= (ends - lengths)[None, :]) & (block[:, None] < ends[None, :])
    first = (ends - lengths) * BLOCK
    inside = 64 * (frame[:, None] - first[None, :])
    span = lengths * BLOCK
    low, high = span_start[0] * span, (span_start[0] + span_size[0]) * span
    masked = jnp.sum(
        (member & (inside >= low[None, :]) & (inside < high[None, :])).astype(F32), axis=1
    )
    level = jnp.sum(jnp.where(member, timestep[0][None, :], 0), axis=1).astype(F32) / 64.0

    frames = bins.reshape(rows, 2 * mel).astype(F32)
    noise, data = frames[:, :mel], frames[:, mel:]
    noisy = (1.0 - level[:, None]) * noise + level[:, None] * data
    cond = data * (1.0 - masked[:, None])
    target = data - noise
    inputs = jnp.concatenate([noisy, cond], axis=1).astype(BF16)
    hidden0 = dot(inputs, in_weight)
    scale = lax.rsqrt(jnp.mean(hidden0 * hidden0, axis=1, keepdims=True) + 1e-06)
    normed = (hidden0 * scale * norm_gain.astype(F32)[None, :]).astype(BF16)
    query = dot(normed, qkv_weight[:, 0, :]).astype(BF16)
    keys = dot(normed, qkv_weight[:, 1, :]).astype(BF16)
    values = dot(normed, qkv_weight[:, 2, :]).astype(BF16)

    attended = pl.pallas_call(
        functools.partial(attend_kernel, longest),
        out_shape=jax.ShapeDtypeStruct((rows, width), BF16),
        in_specs=[SMEM] + [VMEM] * 3,
        out_specs=VMEM,
        compiler_params=params(),
        name="attend",
    )(utt_blocks, query, keys, values)
    everyone = pl.pallas_call(
        functools.partial(gather_kernel, dp, mp),
        out_shape=jax.ShapeDtypeStruct((mp, rows, width), BF16),
        in_specs=[VMEM],
        out_specs=VMEM,
        scratch_shapes=[dma(()), dma((mp,)), dma((mp,)), dma((mp,)), dma((mp,))],
        compiler_params=params(collective_id=1, has_side_effects=True),
        name="gather_attended",
    )(attended)
    mixed = None
    for g in range(mp):
        part = dot(everyone[g], out_full[g * width : (g + 1) * width]).astype(BF16).astype(F32)
        mixed = part if mixed is None else mixed + part
    hidden1 = (hidden0 + mixed).astype(BF16)
    wide1 = lax.optimization_barrier(hidden1).astype(F32)
    rscale = lax.rsqrt(jnp.mean(wide1 * wide1, axis=1, keepdims=True) + 1e-06)
    normalized = wide1 * rscale
    gain_out = final_gain.astype(F32)[None, :]
    final = (normalized * gain_out).astype(BF16)
    velocity = dot(final, vel_weight)
    error = (2.0 * masked[:, None] * (velocity - target)).astype(BF16)
    grad_final = dot(error, vel_weight.T)
    scaled = grad_final * gain_out
    back1 = (
        rscale * (scaled - normalized * jnp.mean(scaled * normalized, axis=1, keepdims=True))
    ).astype(BF16)
    back_att = dot(back1, out_proj.T).astype(BF16)
    grads = pl.pallas_call(
        functools.partial(pullback_kernel, longest),
        out_shape=jax.ShapeDtypeStruct((rows, 3 * width), BF16),
        in_specs=[SMEM] + [VMEM] * 4,
        out_specs=VMEM,
        scratch_shapes=[pltpu.VMEM((rows, width), F32)] * 2,
        compiler_params=params(),
        name="attend_pullback",
    )(utt_blocks, query, keys, values, back_att)
    out_terms = dot(back1, attended, TN).astype(BF16)
    qkv_terms = dot(normed, grads, TN).astype(BF16)
    share = features // dp
    summed_qkv, summed_out = pl.pallas_call(
        functools.partial(reduce_kernel, dp, mp),
        out_shape=(
            jax.ShapeDtypeStruct((share, 3 * width), F32),
            jax.ShapeDtypeStruct((share, width), F32),
        ),
        in_specs=[VMEM] * 2,
        out_specs=(VMEM,) * 2,
        scratch_shapes=[
            pltpu.VMEM((dp - 1, share, 3 * width), BF16),
            pltpu.VMEM((dp - 1, share, width), BF16),
            dma((dp,)), dma((dp,)), dma((dp,)), dma((dp,)),
        ],
        compiler_params=params(collective_id=2, has_side_effects=True),
        name="reduce_grads",
    )(qkv_terms, out_terms)
    total = count[0, 0]
    return (summed_qkv.reshape(share, 3, width) / total, summed_out.T / total)


def solution(mesh):
    in_specs = (
        P("dp", None), P("dp", None), P(), P("dp", None), P("dp", None), P("dp", None),
        P("dp", None), P(), P(), P(None, None, "mp"), P("mp", None), P(), P(),
    )
    out_specs = (P("dp", None, "mp"), P("mp", "dp"))
    return jax.shard_map(
        functools.partial(shards, mesh.shape["dp"], mesh.shape["mp"]),
        mesh=mesh, in_specs=in_specs, out_specs=out_specs, check_vma=False,
    )
```

time: 273 us -> 127 us (0.47)
  the two profiles are of different devices: /device:TPU:0 before, /device:TPU:13 now
where the time goes in v1:
time: 127 us; the launch traced here: 126 us
  Pallas kernels  80.8 us (64%)
  matrix products  22.1 us (17%)
  other arithmetic  14.5 us (11%)
  local copies, waits for them, and re-layouts  8.04 us (6%)
    pallas_call x1, Pallas kernels, shards(): pl.pallas_call(functools.partial(reduce_kernel, dp, mp), out_shape=(jax.S...  29 us
    dot_general x12, matrix products, dot(): return lax.dot_general(a, b, dims, preferred_element_type=F32)  22.1 us
    pallas_call x1, Pallas kernels, shards(): pl.pallas_call(functools.partial(load_kernel, dp, mp), out_shape=(jax.Sha...  18.9 us
    pallas_call x1, Pallas kernels, shards(): pl.pallas_call(functools.partial(gather_kernel, dp, mp), out_shape=jax.Sh...  12.8 us
    pallas_call x1, Pallas kernels, shards(): pl.pallas_call(functools.partial(pullback_kernel, longest), out_shape=jax...  11.6 us
    pallas_call x1, Pallas kernels, shards(): pl.pallas_call(functools.partial(attend_kernel, longest), out_shape=jax.S...  8.51 us
    convert_element_type x1, other arithmetic, shards(): back1 = (rscale * (scaled - normalized * jnp.mean(scaled * normalized, ax...  3.15 us
    div x2, other arithmetic, shards(): return (summed_qkv.reshape(share, 3, width) / total, summed_out.T / total)  3.09 us

profile of v1, /device:TPU:13, one launch (start us, length us, event | category | flops | bytes accessed | tf_op | source)
XLA Modules:
  0.0 126.4 jit_solution(10538970476771596441)
XLA Ops:
  0.6 0.0 copy-start
  0.6 0.9 reduce-window.4
  1.5 0.7 fusion.59
  2.2 0.1 convert_reduce_fusion
  2.3 0.7 select_reduce_fusion
  3.1 0.7 and_select_fusion.1
  3.8 0.6 select_reduce_fusion.2.pick_ref
  4.5 1.3 %select_reduce_fusion.1.from_ref = s32[8]{0:T(128)} fusion(s32[64]{0:T(128)S(1)} %and_select_fusion, s32[64]{0:T(128)} %param.15, s32[8]{0:T(128)S(1)} %iota_add_fusion), kind=kLoop, calls=%fused_computation.76 | loop fusion | flops 1528 | bytes 576 | tf_op jit(solution)/shard_map/reduce_sum | solution.py:269
  5.8 1.9 %reshape.100 = bf16[8,128,100]{2,1,0:T(8,128)(2,1)S(1)} reshape(bf16[8,12800]{1,0:T(8,128)(2,1)} %param.14) | data formatting | bytes 409600 | tf_op jit(solution)/shard_map/reshape | solution.py:273
  7.7 1.9 %reshape.99 = bf16[8,128,100]{2,1,0:T(8,128)(2,1)S(1)} reshape(bf16[8,12800]{1,0:T(8,128)(2,1)} %param.13) | data formatting | bytes 409600 | tf_op jit(solution)/shard_map/reshape | solution.py:273
  9.6 1.0 pad_maximum_fusion.x_ref
  10.7 18.9 %load_blocks.1 = (bf16[8,128,200]{2,1,0:T(8,128)(2,1)}, bf16[512,1024]{1,0:T(8,128)(2,1)}, f32[8,128]{1,0:T(8,128)}) custom-call(s32[8]{0:T(128)} %select_reduce_fusion.2.pick_ref, s32[8]{0:T(128)} %select_reduce_fusion.1.from_ref, s32[1,4]{1,0:T(1,128)} %utt_ref.5, s32[1,4]{1,0:T(1,128)} %start_ref.1, s32[1,4]{1,0:T(1,128)} %size_ref.1, ...), custom_call_target="tpu_custom_call" | custom-call | tf_op jit(solution)/shard_map/load_blocks/pallas_call | solution.py:276
  29.5 1.1 bitcast_convert_fusion
  30.7 0.2 fusion.61
  30.9 0.0 copy-start.7
  30.9 0.2 copy.41
  31.1 0.2 copy.42
  31.3 0.1 add_convert_fusion.1
  31.4 0.0 copy-done
  31.4 0.8 multiply_reduce_fusion
  32.2 0.0 copy-start.9
  32.3 0.0 copy-done.7
  32.3 0.4 multiply_convert_fusion
  32.7 0.7 copy-done.9
  33.4 0.0 copy-start.3
  33.4 1.5 %convolution_convert_fusion.3.v_ref = bf16[1024,128]{1,0:T(8,128)(2,1)} fusion(bf16[1024,1024]{0,1:T(8,128)(2,1)S(1)} %multiply_convert_fusion, bf16[1024,3,128]{2,0,1:T(8,128)(2,1)S(1)} %copy-done.9), kind=kOutput, calls=%fused_computation.22 | convolution fusion | flops 268566528 | bytes 2621440 | tf_op jit(solution)/shard_map/dot_general | solution.py:21
  34.9 1.5 %convolution_convert_fusion.4.k_ref = bf16[1024,128]{1,0:T(8,128)(2,1)} fusion(bf16[1024,1024]{0,1:T(8,128)(2,1)S(1)} %multiply_convert_fusion, bf16[1024,3,128]{2,0,1:T(8,128)(2,1)S(1)} %copy-done.9), kind=kOutput, calls=%fused_computation.23 | convolution fusion | flops 268566528 | bytes 2621440 | tf_op jit(solution)/shard_map/dot_general | solution.py:21
  36.3 0.0 copy-done.3
  36.3 0.0 copy-start.5
  36.3 1.5 %convolution_convert_fusion.5.q_ref = bf16[1024,128]{1,0:T(8,128)(2,1)} fusion(bf16[1024,1024]{0,1:T(8,128)(2,1)S(1)} %multiply_convert_fusion, bf16[1024,3,128]{2,0,1:T(8,128)(2,1)S(1)} %copy-done.9), kind=kOutput, calls=%fused_computation.24 | convolution fusion | flops 268566528 | bytes 2621440 | tf_op jit(solution)/shard_map/dot_general | solution.py:21
  37.8 8.5 %attend.1.a_ref = bf16[1024,128]{1,0:T(8,128)(2,1)} custom-call(s32[1,4]{1,0:T(1,128)} %utt_ref.5, bf16[1024,128]{1,0:T(8,128)(2,1)} %convolution_convert_fusion.5.q_ref, bf16[1024,128]{1,0:T(8,128)(2,1)} %convolution_convert_fusion.4.k_ref, bf16[1024,128]{1,0:T(8,128)(2,1)} %convolution_convert_fusion.3.v_ref), custom_call_target="tpu_custom_call" | custom-call | tf_op jit(solution)/shard_map/attend/pallas_call | solution.py:323
  46.3 12.8 %gather_attended.1 = bf16[4,1024,128]{2,1,0:T(8,128)(2,1)} custom-call(bf16[1024,128]{1,0:T(8,128)(2,1)} %attend.1.a_ref), custom_call_target="tpu_custom_call" | custom-call | tf_op jit(solution)/shard_map/gather_attended/pallas_call | solution.py:331
  59.1 0.0 copy-start.1
  59.1 0.0 copy-done.5
  59.2 1.8 %fusion.35 = bf16[1024,1024]{0,1:T(8,128)(2,1)S(1)} fusion(bf16[512,1024]{1,0:T(8,128)(2,1)S(1)} %copy-done.5, bf16[4,1024,128]{2,1,0:T(8,128)(2,1)} %gather_attended.1), kind=kOutput, calls=%fused_computation.41 | convolution fusion | flops 268435456 | bytes 2621440 | tf_op jit(solution)/shard_map/dot_general | solution.py:21
  60.9 1.7 %fusion.33 = bf16[1024,1024]{0,1:T(8,128)(2,1)S(1)} fusion(bf16[512,1024]{1,0:T(8,128)(2,1)S(1)} %copy-done.5, bf16[4,1024,128]{2,1,0:T(8,128)(2,1)} %gather_attended.1), kind=kOutput, calls=%fused_computation.39 | convolution fusion | flops 268435456 | bytes 2621440 | tf_op jit(solution)/shard_map/dot_general | solution.py:21
  62.7 0.0 copy-done.1
  62.7 0.8 fusion.31
  63.4 0.0 copy-start.8
  63.4 2.1 %add_convert_fusion = bf16[1024,1024]{0,1:T(8,128)(2,1)S(1)} fusion(f32[1024,1024]{0,1:T(8,128)S(1)} %get-tuple-element.33, bf16[1024,1024]{0,1:T(8,128)(2,1)S(1)} %fusion.31, bf16[1024,1024]{0,1:T(8,128)(2,1)S(1)} %fusion.33, bf16[1024,1024]{0,1:T(8,128)(2,1)S(1)} %fusion.35, bf16[512,1024]{1,0:T(8,128)(2,1)} %get-tuple-element.8, ...), kind=kOutput, calls=%fused_computation.11 | convolution fusion | flops 278921216 | bytes 13107200 | tf_op jit(solution)/shard_map/dot_general | solution.py:21
  65.6 0.5 fusion.8
  66.1 0.0 copy-done.8
  66.1 4.4 %fusion.4 = (f32[1024]{0:T(1024)S(1)}, f32[1024,1024]{0,1:T(8,128)}) fusion(bf16[1024,1024]{0,1:T(8,128)(2,1)S(1)} %add_convert_fusion, f32[1024]{0:T(1024)S(1)} %convert_element_type.105, f32[1024]{0:T(1024)S(1)} %add_rsqrt_fusion, bf16[1024,100]{0,1:T(8,128)(2,1)} %param.25, f32[1024,100]{0,1:T(8,128)S(1)} %copy.42, f32[1024,100]{0,1:T(8,128)S(1)} %copy.41, ...), kind=kOutput, calls=%fused_computation.6 | convolution fusion | flops 429276160 | bytes 7331840 | tf_op jit(solution)/shard_map/dot_general | solution.py:21
  70.5 0.0 copy-start.2
  70.5 0.0 copy-start.6
  70.5 3.2 %fusion.7 = bf16[1024,1024]{0,1:T(8,128)(2,1)S(1)} fusion(bf16[1024,1024]{0,1:T(8,128)(2,1)S(1)} %add_convert_fusion, f32[1024,1024]{0,1:T(8,128)} %get-tuple-element.35, f32[1024]{0:T(1024)S(1)} %broadcast_multiply_fusion.1, f32[1024]{0:T(1024)S(1)} %convert_element_type.105, f32[1024]{0:T(1024)S(1)} %add_rsqrt_fusion), kind=kLoop, calls=%fused_computation.9 | loop fusion | flops 7340032 | bytes 8400896 | tf_op jit(solution)/shard_map/convert_element_type | solution.py:356
  73.6 0.0 copy-done.2
  73.6 0.0 copy-start.4
  73.7 1.4 %convolution_convert_fusion.1.o_ref = bf16[1024,128]{1,0:T(8,128)(2,1)} fusion(bf16[1024,1024]{0,1:T(8,128)(2,1)S(1)} %fusion.7, bf16[1024,128]{1,0:T(8,128)(2,1)S(1)} %copy-done.2), kind=kOutput, calls=%fused_computation.20 | convolution fusion | flops 268566528 | bytes 2621440 | tf_op jit(solution)/shard_map/dot_general | solution.py:21
  75.1 0.0 copy-done.6
  75.1 1.5 %convolution_convert_fusion.2.do_ref = bf16[1024,128]{1,0:T(8,128)(2,1)} fusion(bf16[1024,1024]{0,1:T(8,128)(2,1)S(1)} %fusion.7, bf16[128,1024]{1,0:T(8,128)(2,1)S(1)} %copy-done.6), kind=kOutput, calls=%fused_computation.21 | convolution fusion | flops 268566528 | bytes 2621440 | tf_op jit(solution)/shard_map/dot_general | solution.py:21
  76.6 11.6 %attend_pullback.1 = bf16[1024,384]{1,0:T(8,128)(2,1)} custom-call(s32[1,4]{1,0:T(1,128)} %utt_ref.5, bf16[1024,128]{1,0:T(8,128)(2,1)} %convolution_convert_fusion.5.q_ref, bf16[1024,128]{1,0:T(8,128)(2,1)} %convolution_convert_fusion.4.k_ref, bf16[1024,128]{1,0:T(8,128)(2,1)} %convolution_convert_fusion.3.v_ref, ...), custom_call_target="tpu_custom_call" | custom-call | tf_op jit(solution)/shard_map/attend_pullback/pallas_call | solution.py:358
  88.2 0.0 copy-done.4
  88.2 3.3 %convolution_convert_fusion.qkv_ref = bf16[1024,384]{1,0:T(8,128)(2,1)} fusion(bf16[1024,1024]{0,1:T(8,128)(2,1)S(1)} %copy-done.4, bf16[1024,384]{1,0:T(8,128)(2,1)} %attend_pullback.1), kind=kOutput, calls=%fused_computation.17 | convolution fusion | flops 805699584 | bytes 3670016 | tf_op jit(solution)/shard_map/dot_general | solution.py:21
  91.5 29.0 %reduce_grads.1 = (f32[128,384]{1,0:T(8,128)}, f32[128,128]{1,0:T(8,128)}) custom-call(bf16[1024,384]{1,0:T(8,128)(2,1)} %convolution_convert_fusion.qkv_ref, bf16[1024,128]{1,0:T(8,128)(2,1)} %convolution_convert_fusion.1.o_ref), custom_call_target="tpu_custom_call" | custom-call | tf_op jit(solution)/shard_map/reduce_grads/pallas_call | solution.py:370
  120.5 1.2 slice.55
  121.6 1.5 %divide_bitcast_fusion = f32[128,128]{0,1:T(8,128)S(1)} fusion(f32[128,128]{1,0:T(8,128)} %get-tuple-element.11, f32[]{:T(128)} %bitcast.17), kind=kLoop, calls=%fused_computation.59 | loop fusion | flops 16384 | bytes 131076 | tf_op jit(solution)/shard_map/div | solution.py:387
  123.1 0.7 copy.36
  123.9 1.6 %broadcast_divide_fusion = f32[128,384]{1,0:T(8,128)S(1)} fusion(f32[128,384]{1,0:T(8,128)} %get-tuple-element.9, f32[]{:T(128)} %bitcast.17), kind=kLoop, calls=%fused_computation.58 | loop fusion | flops 49152 | bytes 393220 | tf_op jit(solution)/shard_map/div | solution.py:387
  125.5 0.1 copy.34
  125.6 0.8 copy.35
  (9 shorter events, 0.0 us)
Async XLA Ops:
  0.6 30.8 %copy-start = (bf16[200,1024]{1,0:T(8,128)(2,1)S(1)}, bf16[200,1024]{1,0:T(8,128)(2,1)}, u32[]{:S(2)}) copy-start(bf16[200,1024]{1,0:T(8,128)(2,1)} %param.20) | copy-start | bytes 1228804
  30.9 1.4 %copy-start.7 = (bf16[1024]{0:T(1024)(128)(2,1)S(1)}, bf16[1024]{0:T(1024)(128)(2,1)}, u32[]{:S(2)}) copy-start(bf16[1024]{0:T(1024)(128)(2,1)} %param.21) | copy-start | bytes 6148
  32.2 1.1 copy-start.9
  33.4 3.0 %copy-start.3 = (bf16[1024,1024]{0,1:T(8,128)(2,1)}, bf16[1024,1024]{0,1:T(8,128)(2,1)S(1)}, u32[]{:S(2)}) copy-start(bf16[1024,1024]{0,1:T(8,128)(2,1)S(1)} %multiply_convert_fusion) | copy-start | bytes 6291460
  36.3 22.8 %copy-start.5 = (bf16[512,1024]{1,0:T(8,128)(2,1)S(1)}, bf16[512,1024]{1,0:T(8,128)(2,1)}, u32[]{:S(2)}) copy-start(bf16[512,1024]{1,0:T(8,128)(2,1)} %get-tuple-element.8) | copy-start | bytes 3145732
  59.1 3.5 %copy-start.1 = (bf16[4,1024,128]{2,1,0:T(8,128)(2,1)S(1)}, bf16[4,1024,128]{2,1,0:T(8,128)(2,1)}, u32[]{:S(2)}) copy-start(bf16[4,1024,128]{2,1,0:T(8,128)(2,1)} %gather_attended.1) | copy-start | bytes 3145732
  63.4 2.6 %copy-start.8 = (bf16[1024]{0:T(1024)(128)(2,1)S(1)}, bf16[1024]{0:T(1024)(128)(2,1)}, u32[]{:S(2)}) copy-start(bf16[1024]{0:T(1024)(128)(2,1)} %param.24) | copy-start | bytes 6148
  70.5 3.2 %copy-start.2 = (bf16[1024,128]{1,0:T(8,128)(2,1)S(1)}, bf16[1024,128]{1,0:T(8,128)(2,1)}, u32[]{:S(2)}) copy-start(bf16[1024,128]{1,0:T(8,128)(2,1)} %attend.1.a_ref) | copy-start | bytes 786436
  70.5 4.6 %copy-start.6 = (bf16[128,1024]{1,0:T(8,128)(2,1)S(1)}, bf16[128,1024]{1,0:T(8,128)(2,1)}, u32[]{:S(2)}) copy-start(bf16[128,1024]{1,0:T(8,128)(2,1)} %w_ref.1) | copy-start | bytes 786436
  73.6 14.5 %copy-start.4 = (bf16[1024,1024]{0,1:T(8,128)(2,1)S(1)}, bf16[1024,1024]{0,1:T(8,128)(2,1)}, u32[]{:S(2)}) copy-start(bf16[1024,1024]{0,1:T(8,128)(2,1)} %copy-done.3) | copy-start | bytes 6291460

commit v2 on v1

v2 whole, which is shorter than its diff:
```python
import functools

import jax
import jax.numpy as jnp
from jax import lax
from jax.experimental import pallas as pl
from jax.experimental.pallas import tpu as pltpu
from jax.sharding import PartitionSpec as P

HEAD_DIM = 64
BLOCK = 128
MESH = pl.DeviceIdType.MESH
VMEM = pl.BlockSpec(memory_space=pltpu.VMEM)
SMEM = pl.BlockSpec(memory_space=pltpu.SMEM)
F32, BF16 = jnp.float32, jnp.bfloat16
NT = (((1,), (1,)), ((), ()))
TN = (((0,), (0,)), ((), ()))


def dot(a, b, dims=(((1,), (0,)), ((), ()))):
    return lax.dot_general(a, b, dims, preferred_element_type=F32)


def params(**kw):
    return pltpu.CompilerParams(vmem_limit_bytes=56 * 2**20, **kw)


def greet(dp, mp, with_dp, with_mp):
    me, my = lax.axis_index("dp"), lax.axis_index("mp")
    barrier = pltpu.get_barrier_semaphore()
    n = 0
    if with_dp:
        for i in range(1, dp):
            pl.semaphore_signal(
                barrier, inc=1, device_id=(lax.rem(me + i, dp), my), device_id_type=MESH
            )
        n += dp - 1
    if with_mp:
        for i in range(1, mp):
            pl.semaphore_signal(
                barrier, inc=1, device_id=(me, lax.rem(my + i, mp)), device_id_type=MESH
            )
        n += mp - 1
    return lambda: pl.semaphore_wait(barrier, n)


def gather_mp(mp, src, dst_at, local, send, recv, fsend, frecv):
    me, my = lax.axis_index("dp"), lax.axis_index("mp")
    pair, side = my // 2, lax.rem(my, 2)
    mate = pair * 2 + 1 - side
    keep = pltpu.make_async_copy(src, dst_at(my), local)
    direct = []
    for c in range(1, mp // 2):
        far = lax.rem(pair + c, mp // 2) * 2 + side
        direct.append(
            pltpu.make_async_remote_copy(
                src, dst_at(my), send.at[c], recv.at[c], device_id=(me, far), device_id_type=MESH
            )
        )
    near = pltpu.make_async_remote_copy(
        src, dst_at(my), send.at[0], recv.at[0], device_id=(me, mate), device_id_type=MESH
    )

    def start():
        for d in direct:
            d.start()
        near.start()
        keep.start()

    def finish():
        onward = []
        for c, d in enumerate(direct, 1):
            d.wait_recv()
            origin = lax.rem(pair + mp // 2 - c, mp // 2) * 2 + side
            f = pltpu.make_async_remote_copy(
                dst_at(origin), dst_at(origin), fsend.at[c], frecv.at[c],
                device_id=(me, mate), device_id_type=MESH,
            )
            f.start()
            onward.append(f)
        near.wait()
        keep.wait()
        for d in direct:
            d.wait_send()
        for f in onward:
            f.wait()

    return start, finish


def load_kernel(
    dp, mp, dest_ref, utt_ref, start_ref, size_ref, x_ref, w_ref,
    bin_ref, full_ref, count_ref,
    stage, got, tally, send, recv, csend, crecv, hsend, hrecv, local, ssend, srecv, fsend, frecv,
):
    me, my = lax.axis_index("dp"), lax.axis_index("mp")
    wait = greet(dp, mp, True, True)
    per_dev = bin_ref.shape[1]
    owners = [dest_ref[me * per_dev + k] // per_dev for k in range(per_dev)]
    for i in range(dp):
        to = lax.rem(me + i, dp)
        pick = jnp.int32(0)
        for k in range(per_dev):
            pick = jnp.where(owners[k] == to, k, pick)
        for part in range(2):
            stage[i, part] = x_ref[part, pick]
    count = jnp.int32(0)
    for u in range(utt_ref.shape[1]):
        low = start_ref[0, u]
        high = jnp.minimum(low + size_ref[0, u], 64)
        count += (high - low) * utt_ref[0, u] * (BLOCK // 64)
    tally[me] = jnp.full(tally.shape[1:], count, jnp.int32).astype(F32)
    side = lax.rem(my, 2)
    mate = my + 1 - 2 * side
    half = BLOCK // 2
    lines = pl.ds(pl.multiple_of(side * half, half), half)
    got[me, :, lines] = stage[0, :, lines]
    wait()
    rows = w_ref.shape[0]
    start, finish = gather_mp(
        mp, w_ref, lambda i: full_ref.at[pl.ds(pl.multiple_of(i * rows, rows), rows)],
        local, ssend, srecv, fsend, frecv,
    )
    frames, counts = [], []
    for i in range(1, dp):
        to = lax.rem(me + i, dp)
        frames.append(
            pltpu.make_async_remote_copy(
                stage.at[i, :, lines], got.at[me, :, lines], send.at[i], recv.at[i],
                device_id=(to, my), device_id_type=MESH,
            )
        )
        counts.append(
            pltpu.make_async_remote_copy(
                tally.at[me], tally.at[me], csend.at[i], crecv.at[i],
                device_id=(to, my), device_id_type=MESH,
            )
        )
    for c in frames + counts:
        c.start()
    start()
    onward = []
    for i in range(dp):
        if i > 0:
            frames[i - 1].wait_recv()
        slot = lax.rem(me + dp - i, dp)
        f = pltpu.make_async_remote_copy(
            got.at[slot, :, lines], got.at[slot, :, lines], hsend.at[i], hrecv.at[i],
            device_id=(me, mate), device_id_type=MESH,
        )
        f.start()
        onward.append(f)

    def find(i, found):
        d = dest_ref[i]
        return tuple(jnp.where(d == me * per_dev + j, i // per_dev, o) for j, o in enumerate(found))

    origin = lax.fori_loop(0, dp * per_dev, find, (jnp.int32(0),) * per_dev)
    finish()
    for c in frames:
        c.wait_send()
    for c in counts + onward:
        c.wait()
    for j in range(per_dev):
        for part in range(2):
            bin_ref[part, j] = got[origin[j], part]
    count_ref[...] = jnp.sum(tally[...], axis=0)


def gather_kernel(dp, mp, a_ref, out_ref, local, send, recv, fsend, frecv):
    greet(dp, mp, False, True)()
    start, finish = gather_mp(mp, a_ref, lambda i: out_ref.at[i], local, send, recv, fsend, frecv)
    start()
    finish()


def reduce_kernel(
    dp, mp, normed_ref, d_ref, back_ref, att_ref, count_ref, qkv_out, o_out,
    terms, near, sums, far, s1, r1, s2, r2,
):
    me, my = lax.axis_index("dp"), lax.axis_index("mp")
    ready = greet(dp, mp, True, False)
    rows, chunks, groups = o_out.shape[0], terms.shape[0], dp // 2
    group, side = me // 2, lax.rem(me, 2)
    mate = me + 1 - 2 * side
    width = o_out.shape[1]

    def block(j, g, s):
        return terms.at[j, pl.ds(pl.multiple_of((g * 2 + s) * rows, rows), rows)]

    first, second = [], []
    for j in range(chunks):
        if j == 0:
            t = dot(back_ref[...], att_ref[...], TN)
        else:
            t = dot(normed_ref[...], d_ref[:, (j - 1) * width : j * width], TN)
        terms[j] = t.astype(BF16)
        if j == 0:
            ready()
        out = []
        for i in range(groups):
            g = lax.rem(group + i, groups)
            out.append(
                pltpu.make_async_remote_copy(
                    block(j, g, 1 - side), near.at[j, g], s1.at[j, i], r1.at[j, i],
                    device_id=(mate, my), device_id_type=MESH,
                )
            )
        for c in out[1:] + out[:1]:
            c.start()
        first.append(out)

    def middle(j):
        for i in range(1, groups):
            g = lax.rem(group + i, groups)
            first[j][i].wait_recv()
            sums[j, i] = (block(j, g, side)[...].astype(F32) + near[j, g].astype(F32)).astype(BF16)
            c = pltpu.make_async_remote_copy(
                sums.at[j, i], far.at[j, i], s2.at[j, i], r2.at[j, i],
                device_id=(g * 2 + side, my), device_id_type=MESH,
            )
            c.start()
            second.append(c)
        first[j][0].wait_recv()

    def last(j):
        total = block(j, group, side)[...].astype(F32) + near[j, group].astype(F32)
        for i in range(1, groups):
            second[j * (groups - 1) + i - 1].wait_recv()
            total += far[j, i].astype(F32)
        total = total / count_ref[0:1, :]
        if j == 0:
            o_out[...] = total
        else:
            qkv_out[:, (j - 1) * width : j * width] = total

    for j in range(chunks):
        middle(j)
    for j in range(chunks):
        last(j)
    for out in first:
        for c in out:
            c.wait_send()
    for c in second:
        c.wait_send()


def utterances(utt_ref, longest, body):
    def step(u, at):
        length = utt_ref[0, u]
        for n in range(1, longest + 1):
            @pl.when(length == n)
            def _():
                body(pl.ds(pl.multiple_of(at * BLOCK, BLOCK), n * BLOCK))
        return at + length

    lax.fori_loop(0, utt_ref.shape[1], step, jnp.int32(0))


def span_table(utt_ref, start_ref, size_ref, step_ref, b):
    at = jnp.int32(0)
    offset = low = high = step = jnp.int32(0)
    for u in range(utt_ref.shape[1]):
        n = utt_ref[0, u]
        inside = (b >= at) & (b < at + n)
        lo = start_ref[0, u] * n * (BLOCK // 64)
        hi = (start_ref[0, u] + size_ref[0, u]) * n * (BLOCK // 64)
        offset = jnp.where(inside, (b - at) * BLOCK, offset)
        low = jnp.where(inside, lo, low)
        high = jnp.where(inside, hi, high)
        if step_ref is not None:
            step = jnp.where(inside, step_ref[0, u], step)
        at = at + n
    frame = offset + lax.broadcasted_iota(jnp.int32, (BLOCK, 1), 0)
    masked = ((frame >= low) & (frame < high)).astype(F32)
    return masked, step


def head_masks(width):
    lane = lax.broadcasted_iota(jnp.int32, (1, width), 1) // HEAD_DIM
    return [lane == h for h in range(width // HEAD_DIM)]


def softmax(s):
    e = jnp.exp(s - jnp.max(s, axis=1, keepdims=True))
    return e / jnp.sum(e, axis=1, keepdims=True)


def forward_kernel(
    longest, utt_ref, start_ref, size_ref, step_ref, bin_ref, win_ref, gain_ref, wqkv_ref,
    hidden_ref, normed_ref, qkv_ref, att_ref,
):
    width = att_ref.shape[1]
    gain = gain_ref[...].astype(F32)

    def block(b, _):
        rows = pl.ds(pl.multiple_of(b * BLOCK, BLOCK), BLOCK)
        masked, step = span_table(utt_ref, start_ref, size_ref, step_ref, b)
        noise, data = bin_ref[0, b].astype(F32), bin_ref[1, b].astype(F32)
        level = jnp.full((1, 1), step, jnp.int32).astype(F32) / 64.0
        noisy = (1.0 - level) * noise + level * data
        cond = data * (1.0 - masked)
        inputs = jnp.concatenate([noisy, cond], axis=1).astype(BF16)
        hidden = dot(inputs, win_ref[...])
        hidden_ref[rows] = hidden
        scale = lax.rsqrt(jnp.mean(hidden * hidden, axis=1, keepdims=True) + 1e-06)
        normed = (hidden * scale * gain).astype(BF16)
        normed_ref[rows] = normed
        qkv_ref[rows] = dot(normed, wqkv_ref[...]).astype(BF16)
        return 0

    lax.fori_loop(0, bin_ref.shape[1], block, 0, unroll=2)
    masks = head_masks(width)

    def attend(rows):
        q = qkv_ref[rows, :width] * BF16(HEAD_DIM**-0.5)
        k, v = qkv_ref[rows, width : 2 * width], qkv_ref[rows, 2 * width :]
        out = None
        for m in masks:
            p = softmax(dot(jnp.where(m, q, BF16(0)), k, NT)).astype(BF16)
            o = dot(p, v)
            out = o if out is None else jnp.where(m, o, out)
        att_ref[rows] = out.astype(BF16)

    utterances(utt_ref, longest, attend)


def backward_kernel(
    longest, utt_ref, start_ref, size_ref, bin_ref, hidden_ref, all_ref, out_ref, own_ref, gain_ref,
    vel_ref, qkv_ref, back_ref, d_ref, do_ref,
):
    width = own_ref.shape[0]
    gain = gain_ref[...].astype(F32)

    def block(b, _):
        rows = pl.ds(pl.multiple_of(b * BLOCK, BLOCK), BLOCK)
        masked, _ = span_table(utt_ref, start_ref, size_ref, None, b)
        mixed = None
        for g in range(all_ref.shape[0]):
            part = dot(all_ref[g, rows], out_ref[g * width : (g + 1) * width]).astype(BF16).astype(F32)
            mixed = part if mixed is None else mixed + part
        wide = (hidden_ref[rows] + mixed).astype(BF16).astype(F32)
        rscale = lax.rsqrt(jnp.mean(wide * wide, axis=1, keepdims=True) + 1e-06)
        normalized = wide * rscale
        velocity = dot((normalized * gain).astype(BF16), vel_ref[...])
        target = bin_ref[1, b].astype(F32) - bin_ref[0, b].astype(F32)
        error = (2.0 * masked * (velocity - target)).astype(BF16)
        scaled = dot(error, vel_ref[...], NT) * gain
        back = (
            rscale * (scaled - normalized * jnp.mean(scaled * normalized, axis=1, keepdims=True))
        ).astype(BF16)
        back_ref[rows] = back
        do_ref[rows] = dot(back, own_ref[...], NT).astype(BF16)
        return 0

    lax.fori_loop(0, bin_ref.shape[1], block, 0, unroll=2)
    masks = head_masks(width)
    scale = HEAD_DIM**-0.5

    def pullback(rows):
        q = qkv_ref[rows, :width] * BF16(scale)
        k, v = qkv_ref[rows, width : 2 * width], qkv_ref[rows, 2 * width :]
        do = do_ref[rows]
        dq = dk = dv = None
        for m in masks:
            qh = jnp.where(m, q, BF16(0))
            doh = jnp.where(m, do, BF16(0))
            p = softmax(dot(qh, k, NT))
            dp = dot(doh, v, NT).astype(BF16).astype(F32)
            ds = (p * (dp - jnp.sum(dp * p, axis=1, keepdims=True))).astype(BF16)
            a, b, c = dot(ds, k), dot(ds, qh, TN), dot(p.astype(BF16), doh, TN)
            dq = a if dq is None else jnp.where(m, a, dq)
            dk = b if dk is None else dk + b
            dv = c if dv is None else dv + c
        d_ref[rows, :width] = (dq * scale).astype(BF16)
        d_ref[rows, width : 2 * width] = dk.astype(BF16)
        d_ref[rows, 2 * width :] = dv.astype(BF16)

    utterances(utt_ref, longest, pullback)


def shards(
    dp, mp, noise_blocks, data_blocks, destination, utt_blocks, span_start, span_size, timestep,
    in_weight, norm_gain, qkv_weight, out_proj, final_gain, vel_weight,
):
    per_dev = noise_blocks.shape[0]
    rows = per_dev * BLOCK
    mel = noise_blocks.shape[1] // BLOCK
    lanes = -(-mel // 128) * 128
    features = in_weight.shape[1]
    width = qkv_weight.shape[2]
    longest = min(4, per_dev)
    both = jnp.concatenate([noise_blocks, data_blocks], axis=0).reshape(2, per_dev, BLOCK, mel)
    frames = jnp.pad(both, ((0, 0), (0, 0), (0, 0), (0, lanes - mel)))
    entry = jnp.pad(in_weight.reshape(2, mel, features), ((0, 0), (0, lanes - mel), (0, 0)))
    entry = entry.reshape(2 * lanes, features)
    exit_weight = jnp.pad(vel_weight, ((0, 0), (0, lanes - mel)))
    flat_qkv = qkv_weight.reshape(features, 3 * width)
    dma = pltpu.SemaphoreType.DMA

    def array(shape, kind):
        return jax.ShapeDtypeStruct(shape, kind)

    bins, out_full, count = pl.pallas_call(
        functools.partial(load_kernel, dp, mp),
        out_shape=(
            array(frames.shape, BF16), array((mp * width, features), BF16), array((8, 128), F32),
        ),
        in_specs=[SMEM] * 4 + [VMEM] * 2,
        out_specs=(VMEM,) * 3,
        scratch_shapes=[
            pltpu.VMEM((dp, 2, BLOCK, lanes), BF16),
            pltpu.VMEM((dp, 2, BLOCK, lanes), BF16),
            pltpu.VMEM((dp, 8, 128), F32),
        ] + [dma((dp,))] * 6 + [dma(())] + [dma((mp,))] * 4,
        compiler_params=params(collective_id=0, has_side_effects=True),
        name="load_blocks",
    )(destination, utt_blocks, span_start, span_size, frames, out_proj)
    hidden0, normed, qkv, attended = pl.pallas_call(
        functools.partial(forward_kernel, longest),
        out_shape=(
            array((rows, features), F32), array((rows, features), BF16),
            array((rows, 3 * width), BF16), array((rows, width), BF16),
        ),
        in_specs=[SMEM] * 4 + [VMEM] * 4,
        out_specs=(VMEM,) * 4,
        compiler_params=params(),
        name="forward",
    )(utt_blocks, span_start, span_size, timestep, bins, entry, norm_gain.reshape(1, features), flat_qkv)
    everyone = pl.pallas_call(
        functools.partial(gather_kernel, dp, mp),
        out_shape=array((mp, rows, width), BF16),
        in_specs=[VMEM],
        out_specs=VMEM,
        scratch_shapes=[dma(()), dma((mp,)), dma((mp,)), dma((mp,)), dma((mp,))],
        compiler_params=params(collective_id=1, has_side_effects=True),
        name="gather_attended",
    )(attended)
    back1, grads = pl.pallas_call(
        functools.partial(backward_kernel, longest),
        out_shape=(array((rows, features), BF16), array((rows, 3 * width), BF16)),
        in_specs=[SMEM] * 3 + [VMEM] * 8,
        out_specs=(VMEM,) * 2,
        scratch_shapes=[pltpu.VMEM((rows, width), BF16)],
        compiler_params=params(),
        name="backward",
    )(
        utt_blocks, span_start, span_size, bins, hidden0, everyone, out_full, out_proj,
        final_gain.reshape(1, features), exit_weight, qkv,
    )
    share, groups = features // dp, dp // 2
    summed_qkv, summed_out = pl.pallas_call(
        functools.partial(reduce_kernel, dp, mp),
        out_shape=(array((share, 3 * width), F32), array((share, width), F32)),
        in_specs=[VMEM] * 5,
        out_specs=(VMEM,) * 2,
        scratch_shapes=[
            pltpu.VMEM((4, features, width), BF16),
            pltpu.VMEM((4, groups, share, width), BF16),
            pltpu.VMEM((4, groups, share, width), BF16),
            pltpu.VMEM((4, groups, share, width), BF16),
        ] + [dma((4, groups))] * 4,
        compiler_params=params(collective_id=2, has_side_effects=True),
        name="reduce_grads",
    )(normed, grads, back1, attended, count)
    return (summed_qkv.reshape(share, 3, width), summed_out.T)


def solution(mesh):
    in_specs = (
        P("dp", None), P("dp", None), P(), P("dp", None), P("dp", None), P("dp", None),
        P("dp", None), P(), P(), P(None, None, "mp"), P("mp", None), P(), P(),
    )
    out_specs = (P("dp", None, "mp"), P("mp", "dp"))
    return jax.shard_map(
        functools.partial(shards, mesh.shape["dp"], mesh.shape["mp"]),
        mesh=mesh, in_specs=in_specs, out_specs=out_specs, check_vma=False,
    )
```

time: 127 us -> 99.5 us (0.78)
  the two profiles are of different devices: /device:TPU:13 before, /device:TPU:0 now
where the time goes in v2:
time: 99.5 us; the launch traced here: 99.2 us
  Pallas kernels  84.1 us (85%)
  local copies, waits for them, and re-layouts  13.2 us (13%)
  other arithmetic  1.13 us (1%)
    pallas_call x1, Pallas kernels, shards(): pl.pallas_call(functools.partial(reduce_kernel, dp, mp), out_shape=(array...  23.1 us
    pallas_call x1, Pallas kernels, shards(): pl.pallas_call(functools.partial(backward_kernel, longest), out_shape=(ar...  19.3 us
    pallas_call x1, Pallas kernels, shards(): pl.pallas_call(functools.partial(load_kernel, dp, mp), out_shape=(array(f...  17.7 us
    pallas_call x1, Pallas kernels, shards(): pl.pallas_call(functools.partial(forward_kernel, longest), out_shape=(arr...  12.2 us
    pallas_call x1, Pallas kernels, shards(): pl.pallas_call(functools.partial(gather_kernel, dp, mp), out_shape=array(...  11.8 us
    unnamed x8, local copies, waits for them, and re-layouts  3.78 us

profile of v2, /device:TPU:0, one launch (start us, length us, event | category | flops | bytes accessed | tf_op | source)
XLA Modules:
  0.0 99.2 jit_solution(12072286574305605681)
XLA Ops:
  0.6 0.0 copy-start.1
  0.6 1.3 %reshape.28.gain_ref = bf16[1,1024]{1,0:T(2,128)(2,1)} reshape(bf16[1024]{0:T(1024)(128)(2,1)} %param.21) | data formatting | bytes 4096 | tf_op jit(solution)/shard_map/reshape | solution.py:429
  2.0 1.3 %reshape.30.gain_ref = bf16[1,1024]{1,0:T(2,128)(2,1)} reshape(bf16[1024]{0:T(1024)(128)(2,1)} %param.24) | data formatting | bytes 4096 | tf_op jit(solution)/shard_map/reshape | solution.py:449
  3.2 1.1 %copy.21 = bf16[1024,100]{1,0:T(8,128)(2,1)S(1)} copy(bf16[1024,100]{0,1:T(8,128)(2,1)} %param.25) | data formatting | bytes 409600 | tf_op args[12]
  4.4 0.8 pad.14.vel_ref
  5.1 0.0 copy-start
  5.1 1.1 %pad_maximum_fusion = bf16[16,12800]{1,0:T(8,128)(2,1)S(1)} fusion(bf16[8,12800]{1,0:T(8,128)(2,1)} %param.14, bf16[8,12800]{1,0:T(8,128)(2,1)} %param.13), kind=kLoop, calls=%fused_computation | loop fusion | flops 819200 | bytes 819200 | tf_op jit(solution)/shard_map/concatenate | solution.py:393
  6.3 2.0 %reshape.25 = bf16[2,8,128,100]{3,2,1,0:T(8,128)(2,1)S(1)} reshape(bf16[16,12800]{1,0:T(8,128)(2,1)S(1)} %pad_maximum_fusion) | data formatting | bytes 819200 | tf_op jit(solution)/shard_map/reshape | solution.py:393
  8.2 0.9 pad.12.x_ref
  9.2 0.0 copy-done.1
  9.2 0.1 reshape.26
  9.3 0.9 pad.13
  10.2 0.0 copy-done
  10.2 0.3 copy.19
  10.4 1.1 %copy.20.wqkv_ref = bf16[1024,384]{1,0:T(8,128)(2,1)} copy(bf16[1024,384]{0,1:T(8,128)(2,1)S(1)} %bitcast.4) | data formatting | bytes 1572864 | tf_op jit(solution)/shard_map/reshape | solution.py:398
  11.6 17.7 %load_blocks.1 = (bf16[2,8,128,128]{3,2,1,0:T(8,128)(2,1)}, bf16[512,1024]{1,0:T(8,128)(2,1)}, f32[8,128]{1,0:T(8,128)}) custom-call(s32[64]{0:T(128)} %dest_ref.1, s32[1,4]{1,0:T(1,128)} %utt_ref.5, s32[1,4]{1,0:T(1,128)} %start_ref.5, s32[1,4]{1,0:T(1,128)} %size_ref.5, bf16[2,8,128,128]{3,2,1,0:T(8,128)(2,1)} %pad.12.x_ref, bf16[128,1024]{1,0:T(8,128)(2,1)} %own_ref.1), custom_call_target="tpu_custom_call" | custom-call | tf_op jit(solution)/shard_map/load_blocks/pallas_call | solution.py:404
  29.3 12.2 %forward.1 = (f32[1024,1024]{1,0:T(8,128)}, bf16[1024,1024]{1,0:T(8,128)(2,1)}, bf16[1024,384]{1,0:T(8,128)(2,1)}, bf16[1024,128]{1,0:T(8,128)(2,1)}) custom-call(s32[1,4]{1,0:T(1,128)} %utt_ref.5, s32[1,4]{1,0:T(1,128)} %start_ref.5, s32[1,4]{1,0:T(1,128)} %size_ref.5, s32[1,4]{1,0:T(1,128)} %step_ref.1, ...), custom_call_target="tpu_custom_call" | custom-call | tf_op jit(solution)/shard_map/forward/pallas_call | solution.py:419
  41.5 11.8 %gather_attended.1.all_ref = bf16[4,1024,128]{2,1,0:T(8,128)(2,1)} custom-call(bf16[1024,128]{1,0:T(8,128)(2,1)} %get-tuple-element.16.a_ref.att_ref), custom_call_target="tpu_custom_call" | custom-call | tf_op jit(solution)/shard_map/gather_attended/pallas_call | solution.py:430
  53.3 19.3 %backward.1 = (bf16[1024,1024]{1,0:T(8,128)(2,1)}, bf16[1024,384]{1,0:T(8,128)(2,1)}) custom-call(s32[1,4]{1,0:T(1,128)} %utt_ref.5, s32[1,4]{1,0:T(1,128)} %start_ref.5, s32[1,4]{1,0:T(1,128)} %size_ref.5, bf16[2,8,128,128]{3,2,1,0:T(8,128)(2,1)} %get-tuple-element.13.bin_ref, f32[1024,1024]{1,0:T(8,128)} %get-tuple-element.15.hidden_ref, ...), custom_call_target="tpu_custom_call" | custom-call | tf_op jit(solution)/shard_map/backward/pallas_call | solution.py:439
  72.6 23.1 %reduce_grads.1 = (f32[128,384]{1,0:T(8,128)}, f32[128,128]{1,0:T(8,128)}) custom-call(bf16[1024,1024]{1,0:T(8,128)(2,1)} %get-tuple-element.14.normed_ref, bf16[1024,384]{1,0:T(8,128)(2,1)} %get-tuple-element.19.d_ref, bf16[1024,1024]{1,0:T(8,128)(2,1)} %get-tuple-element.20.back_ref, bf16[1024,128]{1,0:T(8,128)(2,1)} %get-tuple-element.16.a_ref.att_ref, ...), custom_call_target="tpu_custom_call" | custom-call | tf_op jit(solution)/shard_map/reduce_grads/pallas_call | solution.py:452
  95.7 1.1 %copy.22 = f32[128,384]{0,1:T(8,128)S(1)} copy(f32[128,384]{1,0:T(8,128)} %get-tuple-element.22) | data formatting | bytes 393216 | tf_op jit(solution)/shard_map/reduce_grads/pallas_call | solution.py:452
  96.8 0.8 copy.23
  97.6 1.6 %copy.24 = f32[128,128]{1,0:T(8,128)} copy(f32[128,128]{0,1:T(8,128)} %bitcast.7) | data formatting | bytes 131072
Async XLA Ops:
  0.6 8.6 %copy-start.1 = (bf16[200,1024]{1,0:T(8,128)(2,1)S(1)}, bf16[200,1024]{1,0:T(8,128)(2,1)}, u32[]{:S(2)}) copy-start(bf16[200,1024]{1,0:T(8,128)(2,1)} %param.20) | copy-start | bytes 1228804
  5.1 5.0 %copy-start = (bf16[1024,3,128]{2,0,1:T(8,128)(2,1)S(1)}, bf16[1024,3,128]{2,0,1:T(8,128)(2,1)}, u32[]{:S(2)}) copy-start(bf16[1024,3,128]{2,0,1:T(8,128)(2,1)} %param.22) | copy-start | bytes 2359300

commit v3 on v2

--- a/solution.py
+++ b/solution.py
@@ -44,43 +44,47 @@
     return lambda: pl.semaphore_wait(barrier, n)
 
 
-def gather_mp(mp, src, dst_at, local, send, recv, fsend, frecv):
+PIECES = 4
+
+
+def gather_mp(mp, src_at, dst_at, local, send, recv, fsend, frecv):
     me, my = lax.axis_index("dp"), lax.axis_index("mp")
     pair, side = my // 2, lax.rem(my, 2)
     mate = pair * 2 + 1 - side
-    keep = pltpu.make_async_copy(src, dst_at(my), local)
-    direct = []
-    for c in range(1, mp // 2):
-        far = lax.rem(pair + c, mp // 2) * 2 + side
-        direct.append(
-            pltpu.make_async_remote_copy(
-                src, dst_at(my), send.at[c], recv.at[c], device_id=(me, far), device_id_type=MESH
-            )
-        )
-    near = pltpu.make_async_remote_copy(
-        src, dst_at(my), send.at[0], recv.at[0], device_id=(me, mate), device_id_type=MESH
-    )
+    direct, keep, near = [], [], []
+    for p in range(PIECES):
+        keep.append(pltpu.make_async_copy(src_at(p), dst_at(my, p), local.at[p]))
+        for c in range(1, mp // 2):
+            far = lax.rem(pair + c, mp // 2) * 2 + side
+            direct.append((p, c, pltpu.make_async_remote_copy(
+                src_at(p), dst_at(my, p), send.at[c, p], recv.at[c, p],
+                device_id=(me, far), device_id_type=MESH,
+            )))
+        near.append(pltpu.make_async_remote_copy(
+            src_at(p), dst_at(my, p), send.at[0, p], recv.at[0, p],
+            device_id=(me, mate), device_id_type=MESH,
+        ))
 
     def start():
-        for d in direct:
+        for _, _, d in direct:
             d.start()
-        near.start()
-        keep.start()
+        for n in near + keep:
+            n.start()
 
     def finish():
         onward = []
-        for c, d in enumerate(direct, 1):
+        for p, c, d in direct:
             d.wait_recv()
             origin = lax.rem(pair + mp // 2 - c, mp // 2) * 2 + side
             f = pltpu.make_async_remote_copy(
-                dst_at(origin), dst_at(origin), fsend.at[c], frecv.at[c],
+                dst_at(origin, p), dst_at(origin, p), fsend.at[c, p], frecv.at[c, p],
                 device_id=(me, mate), device_id_type=MESH,
             )
             f.start()
             onward.append(f)
-        near.wait()
-        keep.wait()
-        for d in direct:
+        for n in near + keep:
+            n.wait()
+        for _, _, d in direct:
             d.wait_send()
         for f in onward:
             f.wait()
@@ -117,8 +121,10 @@
     got[me, :, lines] = stage[0, :, lines]
     wait()
     rows = w_ref.shape[0]
+    piece = rows // PIECES
     start, finish = gather_mp(
-        mp, w_ref, lambda i: full_ref.at[pl.ds(pl.multiple_of(i * rows, rows), rows)],
+        mp, lambda p: w_ref.at[pl.ds(p * piece, piece)],
+        lambda i, p: full_ref.at[pl.ds(pl.multiple_of(i * rows + p * piece, piece), piece)],
         local, ssend, srecv, fsend, frecv,
     )
     frames, counts = [], []
@@ -169,7 +175,11 @@
 
 def gather_kernel(dp, mp, a_ref, out_ref, local, send, recv, fsend, frecv):
     greet(dp, mp, False, True)()
-    start, finish = gather_mp(mp, a_ref, lambda i: out_ref.at[i], local, send, recv, fsend, frecv)
+    piece = a_ref.shape[0] // PIECES
+    start, finish = gather_mp(
+        mp, lambda p: a_ref.at[pl.ds(p * piece, piece)],
+        lambda i, p: out_ref.at[i, pl.ds(p * piece, piece)], local, send, recv, fsend, frecv,
+    )
     start()
     finish()
 
@@ -189,11 +199,36 @@
         return terms.at[j, pl.ds(pl.multiple_of((g * 2 + s) * rows, rows), rows)]
 
     first, second = [], []
+
+    def middle(j):
+        for i in range(1, groups):
+            g = lax.rem(group + i, groups)
+            first[j][i].wait_recv()
+            sums[j, i] = (block(j, g, side)[...].astype(F32) + near[j, g].astype(F32)).astype(BF16)
+            c = pltpu.make_async_remote_copy(
+                sums.at[j, i], far.at[j, i], s2.at[j, i], r2.at[j, i],
+                device_id=(g * 2 + side, my), device_id_type=MESH,
+            )
+            c.start()
+            second.append(c)
+        first[j][0].wait_recv()
+
+    def last(j):
+        total = block(j, group, side)[...].astype(F32) + near[j, group].astype(F32)
+        for i in range(1, groups):
+            second[j * (groups - 1) + i - 1].wait_recv()
+            total += far[j, i].astype(F32)
+        total = total / count_ref[0:1, :]
+        if j == 0:
+            o_out[...] = total.T if o_out.shape[0] == width else total
+        else:
+            qkv_out[j - 1] = total
+
     for j in range(chunks):
         if j == 0:
-            t = dot(back_ref[...], att_ref[...], TN)
+            t = dot(att_ref[...], back_ref[...], TN).T
         else:
-            t = dot(normed_ref[...], d_ref[:, (j - 1) * width : j * width], TN)
+            t = dot(d_ref[:, (j - 1) * width : j * width], normed_ref[...], TN).T
         terms[j] = t.astype(BF16)
         if j == 0:
             ready()
@@ -209,33 +244,9 @@
         for c in out[1:] + out[:1]:
             c.start()
         first.append(out)
-
-    def middle(j):
-        for i in range(1, groups):
-            g = lax.rem(group + i, groups)
-            first[j][i].wait_recv()
-            sums[j, i] = (block(j, g, side)[...].astype(F32) + near[j, g].astype(F32)).astype(BF16)
-            c = pltpu.make_async_remote_copy(
-                sums.at[j, i], far.at[j, i], s2.at[j, i], r2.at[j, i],
-                device_id=(g * 2 + side, my), device_id_type=MESH,
-            )
-            c.start()
-            second.append(c)
-        first[j][0].wait_recv()
-
-    def last(j):
-        total = block(j, group, side)[...].astype(F32) + near[j, group].astype(F32)
-        for i in range(1, groups):
-            second[j * (groups - 1) + i - 1].wait_recv()
-            total += far[j, i].astype(F32)
-        total = total / count_ref[0:1, :]
-        if j == 0:
-            o_out[...] = total
-        else:
-            qkv_out[:, (j - 1) * width : j * width] = total
-
-    for j in range(chunks):
-        middle(j)
+        if j > 0:
+            middle(j - 1)
+    middle(chunks - 1)
     for j in range(chunks):
         last(j)
     for out in first:
@@ -291,7 +302,7 @@
     hidden_ref, normed_ref, qkv_ref, att_ref,
 ):
     width = att_ref.shape[1]
-    gain = gain_ref[...].astype(F32)
+    gain = gain_ref[...].astype(F32).reshape(1, -1)
 
     def block(b, _):
         rows = pl.ds(pl.multiple_of(b * BLOCK, BLOCK), BLOCK)
@@ -306,7 +317,8 @@
         scale = lax.rsqrt(jnp.mean(hidden * hidden, axis=1, keepdims=True) + 1e-06)
         normed = (hidden * scale * gain).astype(BF16)
         normed_ref[rows] = normed
-        qkv_ref[rows] = dot(normed, wqkv_ref[...]).astype(BF16)
+        for j in range(3):
+            qkv_ref[rows, j * width : (j + 1) * width] = dot(normed, wqkv_ref[j]).astype(BF16)
         return 0
 
     lax.fori_loop(0, bin_ref.shape[1], block, 0, unroll=2)
@@ -330,7 +342,7 @@
     vel_ref, qkv_ref, back_ref, d_ref, do_ref,
 ):
     width = own_ref.shape[0]
-    gain = gain_ref[...].astype(F32)
+    gain = gain_ref[...].astype(F32).reshape(1, -1)
 
     def block(b, _):
         rows = pl.ds(pl.multiple_of(b * BLOCK, BLOCK), BLOCK)
@@ -342,10 +354,10 @@
         wide = (hidden_ref[rows] + mixed).astype(BF16).astype(F32)
         rscale = lax.rsqrt(jnp.mean(wide * wide, axis=1, keepdims=True) + 1e-06)
         normalized = wide * rscale
-        velocity = dot((normalized * gain).astype(BF16), vel_ref[...])
+        velocity = dot((normalized * gain).astype(BF16), vel_ref[...], NT)
         target = bin_ref[1, b].astype(F32) - bin_ref[0, b].astype(F32)
         error = (2.0 * masked * (velocity - target)).astype(BF16)
-        scaled = dot(error, vel_ref[...], NT) * gain
+        scaled = dot(error, vel_ref[...]) * gain
         back = (
             rscale * (scaled - normalized * jnp.mean(scaled * normalized, axis=1, keepdims=True))
         ).astype(BF16)
@@ -386,16 +398,10 @@
     per_dev = noise_blocks.shape[0]
     rows = per_dev * BLOCK
     mel = noise_blocks.shape[1] // BLOCK
-    lanes = -(-mel // 128) * 128
     features = in_weight.shape[1]
     width = qkv_weight.shape[2]
     longest = min(4, per_dev)
-    both = jnp.concatenate([noise_blocks, data_blocks], axis=0).reshape(2, per_dev, BLOCK, mel)
-    frames = jnp.pad(both, ((0, 0), (0, 0), (0, 0), (0, lanes - mel)))
-    entry = jnp.pad(in_weight.reshape(2, mel, features), ((0, 0), (0, lanes - mel), (0, 0)))
-    entry = entry.reshape(2 * lanes, features)
-    exit_weight = jnp.pad(vel_weight, ((0, 0), (0, lanes - mel)))
-    flat_qkv = qkv_weight.reshape(features, 3 * width)
+    frames = jnp.concatenate([noise_blocks, data_blocks], axis=0).reshape(2, per_dev, BLOCK, mel)
     dma = pltpu.SemaphoreType.DMA
 
     def array(shape, kind):
@@ -409,10 +415,10 @@
         in_specs=[SMEM] * 4 + [VMEM] * 2,
         out_specs=(VMEM,) * 3,
         scratch_shapes=[
-            pltpu.VMEM((dp, 2, BLOCK, lanes), BF16),
-            pltpu.VMEM((dp, 2, BLOCK, lanes), BF16),
+            pltpu.VMEM((dp, 2, BLOCK, mel), BF16),
+            pltpu.VMEM((dp, 2, BLOCK, mel), BF16),
             pltpu.VMEM((dp, 8, 128), F32),
-        ] + [dma((dp,))] * 6 + [dma(())] + [dma((mp,))] * 4,
+        ] + [dma((dp,))] * 6 + [dma((PIECES,))] + [dma((mp, PIECES))] * 4,
         compiler_params=params(collective_id=0, has_side_effects=True),
         name="load_blocks",
     )(destination, utt_blocks, span_start, span_size, frames, out_proj)
@@ -426,13 +432,13 @@
         out_specs=(VMEM,) * 4,
         compiler_params=params(),
         name="forward",
-    )(utt_blocks, span_start, span_size, timestep, bins, entry, norm_gain.reshape(1, features), flat_qkv)
+    )(utt_blocks, span_start, span_size, timestep, bins, in_weight, norm_gain, qkv_weight.transpose(1, 0, 2))
     everyone = pl.pallas_call(
         functools.partial(gather_kernel, dp, mp),
         out_shape=array((mp, rows, width), BF16),
         in_specs=[VMEM],
         out_specs=VMEM,
-        scratch_shapes=[dma(()), dma((mp,)), dma((mp,)), dma((mp,)), dma((mp,))],
+        scratch_shapes=[dma((PIECES,))] + [dma((mp, PIECES))] * 4,
         compiler_params=params(collective_id=1, has_side_effects=True),
         name="gather_attended",
     )(attended)
@@ -446,12 +452,12 @@
         name="backward",
     )(
         utt_blocks, span_start, span_size, bins, hidden0, everyone, out_full, out_proj,
-        final_gain.reshape(1, features), exit_weight, qkv,
+        final_gain, vel_weight.T, qkv,
     )
     share, groups = features // dp, dp // 2
     summed_qkv, summed_out = pl.pallas_call(
         functools.partial(reduce_kernel, dp, mp),
-        out_shape=(array((share, 3 * width), F32), array((share, width), F32)),
+        out_shape=(array((3, share, width), F32), array((share, width), F32)),
         in_specs=[VMEM] * 5,
         out_specs=(VMEM,) * 2,
         scratch_shapes=[
@@ -463,7 +469,10 @@
         compiler_params=params(collective_id=2, has_side_effects=True),
         name="reduce_grads",
     )(normed, grads, back1, attended, count)
-    return (summed_qkv.reshape(share, 3, width), summed_out.T)
+    return (
+        summed_qkv.transpose(1, 0, 2),
+        summed_out if share == width else summed_out.T,
+    )
 
 
 def solution(mesh):

time: 99.5 us -> 93.1 us (0.936)
  local copies, waits for them, and re-layouts: 13.2 us -> 5.85 us
  Pallas kernels: 84.1 us -> 85.2 us
    reshape x4 -> x0, local copies, waits for them, and re-layouts: 3.83 us -> none  [the longest x1 1.33 us: shards(): norm_gain.reshape(1, features)]
    pad x3 -> x0, local copies, waits for them, and re-layouts: 2.59 us -> none  [the longest x1 0.94 us: shards(): frames = jnp.pad(both, ((0, 0), (0, 0), (0, 0), (0, lanes - mel)))]
    pallas_call x1 -> x0, local copies, waits for them, and re-layouts: 1.05 us -> none  [shards(): pl.pallas_call(functools.partial(reduce_kernel, dp, mp), out_shape=(array...]
    unnamed x8 -> x2, local copies, waits for them, and re-layouts: 3.78 us -> 3.09 us
where the time goes in v3:
time: 93.1 us; the launch traced here: 92.8 us
  Pallas kernels  85.2 us (92%)
  local copies, waits for them, and re-layouts  5.85 us (6%)
  other arithmetic  1.06 us (1%)
    pallas_call x1, Pallas kernels, shards(): pl.pallas_call(functools.partial(reduce_kernel, dp, mp), out_shape=(array...  22.3 us
    pallas_call x1, Pallas kernels, shards(): pl.pallas_call(functools.partial(backward_kernel, longest), out_shape=(ar...  20 us
    pallas_call x1, Pallas kernels, shards(): pl.pallas_call(functools.partial(load_kernel, dp, mp), out_shape=(array(f...  17.9 us
    pallas_call x1, Pallas kernels, shards(): pl.pallas_call(functools.partial(forward_kernel, longest), out_shape=(arr...  12.9 us
    pallas_call x1, Pallas kernels, shards(): pl.pallas_call(functools.partial(gather_kernel, dp, mp), out_shape=array(...  12 us
    unnamed x2, local copies, waits for them, and re-layouts  3.09 us
    reshape x1, local copies, waits for them, and re-layouts, shards(): jnp.concatenate([noise_blocks, data_blocks], axis=0)  2.76 us

profile of v3, /device:TPU:0, one launch (start us, length us, event | category | flops | bytes accessed | tf_op | source)
XLA Modules:
  0.0 92.8 jit_solution(3835981913662065007)
XLA Ops:
  0.6 1.1 %pad_maximum_fusion = bf16[16,12800]{1,0:T(8,128)(2,1)S(1)} fusion(bf16[8,12800]{1,0:T(8,128)(2,1)} %param.14, bf16[8,12800]{1,0:T(8,128)(2,1)} %param.13), kind=kLoop, calls=%fused_computation | loop fusion | flops 819200 | bytes 819200 | tf_op jit(solution)/shard_map/concatenate | solution.py:404
  1.7 2.8 %reshape.7.x_ref = bf16[2,8,128,100]{3,2,1,0:T(8,128)(2,1)} reshape(bf16[16,12800]{1,0:T(8,128)(2,1)S(1)} %pad_maximum_fusion) | data formatting | bytes 819200 | tf_op jit(solution)/shard_map/reshape | solution.py:404
  4.5 17.9 %load_blocks.1 = (bf16[2,8,128,100]{3,2,1,0:T(8,128)(2,1)}, bf16[512,1024]{1,0:T(8,128)(2,1)}, f32[8,128]{1,0:T(8,128)}) custom-call(s32[64]{0:T(128)} %dest_ref.1, s32[1,4]{1,0:T(1,128)} %utt_ref.5, s32[1,4]{1,0:T(1,128)} %start_ref.5, s32[1,4]{1,0:T(1,128)} %size_ref.5, bf16[2,8,128,100]{3,2,1,0:T(8,128)(2,1)} %reshape.7.x_ref, bf16[128,1024]{1,0:T(8,128)(2,1)} %own_ref.1), custom_call_target="tpu_custom_call" | custom-call | tf_op jit(solution)/shard_map/load_blocks/pallas_call | solution.py:410
  22.4 12.9 %forward.1 = (f32[1024,1024]{1,0:T(8,128)}, bf16[1024,1024]{1,0:T(8,128)(2,1)}, bf16[1024,384]{1,0:T(8,128)(2,1)}, bf16[1024,128]{1,0:T(8,128)(2,1)}) custom-call(s32[1,4]{1,0:T(1,128)} %utt_ref.5, s32[1,4]{1,0:T(1,128)} %start_ref.5, s32[1,4]{1,0:T(1,128)} %size_ref.5, s32[1,4]{1,0:T(1,128)} %step_ref.1, ...), custom_call_target="tpu_custom_call" | custom-call | tf_op jit(solution)/shard_map/forward/pallas_call | solution.py:425
  35.3 12.0 %gather_attended.1.all_ref = bf16[4,1024,128]{2,1,0:T(8,128)(2,1)} custom-call(bf16[1024,128]{1,0:T(8,128)(2,1)} %get-tuple-element.16.a_ref.att_ref), custom_call_target="tpu_custom_call" | custom-call | tf_op jit(solution)/shard_map/gather_attended/pallas_call | solution.py:436
  47.3 20.0 %backward.1 = (bf16[1024,1024]{1,0:T(8,128)(2,1)}, bf16[1024,384]{1,0:T(8,128)(2,1)}) custom-call(s32[1,4]{1,0:T(1,128)} %utt_ref.5, s32[1,4]{1,0:T(1,128)} %start_ref.5, s32[1,4]{1,0:T(1,128)} %size_ref.5, bf16[2,8,128,100]{3,2,1,0:T(8,128)(2,1)} %get-tuple-element.13.bin_ref, f32[1024,1024]{1,0:T(8,128)} %get-tuple-element.15.hidden_ref, ...), custom_call_target="tpu_custom_call" | custom-call | tf_op jit(solution)/shard_map/backward/pallas_call | solution.py:445
  67.3 22.3 %reduce_grads.1 = (f32[3,128,128]{2,1,0:T(8,128)}, f32[128,128]{1,0:T(8,128)}) custom-call(bf16[1024,1024]{1,0:T(8,128)(2,1)} %get-tuple-element.14.normed_ref, bf16[1024,384]{1,0:T(8,128)(2,1)} %get-tuple-element.19.d_ref, bf16[1024,1024]{1,0:T(8,128)(2,1)} %get-tuple-element.20.back_ref, bf16[1024,128]{1,0:T(8,128)(2,1)} %get-tuple-element.16.a_ref.att_ref, ...), custom_call_target="tpu_custom_call" | custom-call | tf_op jit(solution)/shard_map/reduce_grads/pallas_call | solution.py:458
  89.7 1.6 %copy.17 = f32[128,3,128]{2,0,1:T(8,128)} copy(f32[128,3,128]{2,0,1:T(8,128)} %bitcast.5) | data formatting | bytes 393216
  91.3 1.5 %copy.18 = f32[128,128]{1,0:T(8,128)} copy(f32[128,128]{1,0:T(8,128)} %get-tuple-element.27) | data formatting | bytes 131072
